TPU v7x, 32 devices: a whole 2x2x4 slice. The times are simulated.
32 devices in a mesh: gx: 8 (over y, x, core), gy: 4 (over z).
Axes of the slice: x: 2, y: 2, z: 4, core: 2. Of those that a mesh axis runs over, the one named last changes fastest.
Arguments:
- adjoint: float32 [9, 32, 128, 512], P(None, 'gx', 'gy'), may hold values from -6 to 6
- buoyancy: float32 [32, 128, 512], P('gx', 'gy'), may hold values from 0.5 to 2
- lame_lambda: float32 [32, 128, 512], P('gx', 'gy'), may hold values from 0.5 to 2
- shear_mu: float32 [32, 128, 512], P('gx', 'gy'), may hold values from 0.3 to 1.2
- packed: int32 [8, 8, 4, 12, 2048], P('gx', None, 'gy'), may hold values from -2147483648 to 2147483646
- scales: float32 [8, 8, 4, 12], P('gx', None, 'gy'), may hold values from 0.005 to 0.05
- perm: int32 [8, 8], P('gx'), may hold values from 0 to 7, each once within a row
Outputs:
- adjoint_out: float32 [9, 32, 128, 512], P(None, 'gx', 'gy')
- gradients: float32 [2, 32, 128, 512], P(None, 'gx', 'gy')
Inputs may be any that keep to these rules, and one draw needn't show every extreme that they name: Each row of perm names every number 0 to 7 once. The words of packed are stored inputs and may cross devices as they are, four signed bytes to a word; only values that a program computes travel in float32.
All inputs are finite; a program needn't handle non-finite values.
Results may differ from a plain program's by a relative error of at most 0.0003.
Values sent between devices are 32-bit elements; how exact they have to be, the bound alone decides.
A program may use at most 128 MiB of HBM per device.

v0:
```python
import jax
import jax.numpy as jnp
from jax import lax
from jax.sharding import PartitionSpec as P

STEPS = 2


courant = 0.15


def passed_along(value, axis, steps):
    count = lax.axis_size(axis)
    first, last = (max(0, -steps), min(count, count - steps))
    return lax.ppermute(value, axis, [(source, source + steps) for source in range(first, last)])


def unpack(words):
    low = (words & 255) - 128
    middle = (jnp.right_shift(words, 8) & 255) - 128
    high = (jnp.right_shift(words, 16) & 255) - 128
    topmost = jnp.right_shift(words, 24)
    return jnp.concatenate([low, middle, high, topmost], axis=-1).astype(jnp.float32)


def inverse_order(row):
    count = row.shape[0]
    slots = jnp.arange(count, dtype=jnp.int32)
    hits = (row[None, :] == slots[:, None]).astype(jnp.int32)
    return jnp.sum(hits * slots[None, :], axis=1)


def frame(field, ahead_x, behind_x, ahead_y, behind_y):
    rows_x, rows_y, rows_z = field.shape
    zero_x = jnp.zeros((1, rows_y, rows_z), jnp.float32)
    lower_x = zero_x if behind_x is None else behind_x
    upper_x = zero_x if ahead_x is None else ahead_x
    middle = jnp.concatenate([lower_x, field, upper_x], axis=0)
    zero_y = jnp.zeros((rows_x, 1, rows_z), jnp.float32)
    lower_y = zero_y if behind_y is None else behind_y
    upper_y = zero_y if ahead_y is None else ahead_y
    lower_y = jnp.pad(lower_y, ((1, 1), (0, 0), (0, 0)))
    upper_y = jnp.pad(upper_y, ((1, 1), (0, 0), (0, 0)))
    joined = jnp.concatenate([lower_y, middle, upper_y], axis=1)
    return jnp.pad(joined, ((0, 0), (0, 0), (1, 1)))


def window(field, margin, out_margin, shift):
    start_x = margin - out_margin + shift[0]
    start_y = margin - out_margin + shift[1]
    start_z = 1 + shift[2]
    size_x = field.shape[0] - 2 * margin + 2 * out_margin
    size_y = field.shape[1] - 2 * margin + 2 * out_margin
    size_z = field.shape[2] - 2
    return lax.slice(
        field, (start_x, start_y, start_z), (start_x + size_x, start_y + size_y, start_z + size_z)
    )


def unit_shift(axis, amount):
    offsets = [0, 0, 0]
    offsets[axis] = amount
    return tuple(offsets)


def diff_ahead(field, axis, margin, out_margin):
    return window(field, margin, out_margin, unit_shift(axis, 1)) - window(
        field, margin, out_margin, (0, 0, 0)
    )


def diff_behind(field, axis, margin, out_margin):
    return window(field, margin, out_margin, (0, 0, 0)) - window(
        field, margin, out_margin, unit_shift(axis, -1)
    )


def move_velocity(velocity, stress, buoyancy, margin, out_margin):
    scaled = courant * buoyancy

    def ahead(field, axis):
        return diff_ahead(field, axis, margin, out_margin)

    def behind(field, axis):
        return diff_behind(field, axis, margin, out_margin)

    return [
        velocity[0] - scaled * (ahead(stress[0], 0) + behind(stress[3], 1) + behind(stress[4], 2)),
        velocity[1] - scaled * (behind(stress[3], 0) + ahead(stress[1], 1) + behind(stress[5], 2)),
        velocity[2] - scaled * (behind(stress[4], 0) + behind(stress[5], 1) + ahead(stress[2], 2)),
    ]


def strains(padded, margin):

    def ahead(field, axis):
        return diff_ahead(field, axis, margin, 0)

    def behind(field, axis):
        return diff_behind(field, axis, margin, 0)

    return [
        behind(padded[0], 0),
        behind(padded[1], 1),
        behind(padded[2], 2),
        ahead(padded[0], 1) + ahead(padded[1], 0),
        ahead(padded[0], 2) + ahead(padded[2], 0),
        ahead(padded[1], 2) + ahead(padded[2], 1),
    ]


def move_stress(stress, strain, lame_lambda, shear_mu):
    trace = strain[0] + strain[1] + strain[2]
    result = []
    for index in range(3):
        result.append(
            stress[index] - courant * (lame_lambda * trace + 2.0 * shear_mu * strain[index])
        )
    for index in range(3, 6):
        result.append(stress[index] - courant * shear_mu * strain[index])
    return result


def on_device(adjoint, buoyancy, lame_lambda, shear_mu, packed, scales, perm):
    cells_x, cells_y, cells_z = buoyancy.shape
    inverse = inverse_order(perm[0])
    words = lax.all_to_all(packed, "gx", split_axis=1, concat_axis=0, tiled=True)
    factor = lax.all_to_all(scales, "gx", split_axis=1, concat_axis=0, tiled=True)
    blocks = unpack(words[:, 0, 0]) * factor[:, 0, 0, :, None]
    ordered = jnp.take(blocks, inverse, axis=0)
    forward = jnp.transpose(ordered, (1, 0, 2)).reshape(blocks.shape[1], cells_x, cells_y, cells_z)
    velocity = [adjoint[index] for index in range(3)]
    stress = [adjoint[index] for index in range(3, 9)]
    grad_lambda = jnp.zeros(buoyancy.shape, jnp.float32)
    grad_mu = jnp.zeros(buoyancy.shape, jnp.float32)
    for step in range(STEPS):
        stress_xx, stress_yy, stress_zz, stress_xy, stress_xz, stress_yz = stress
        next_x = passed_along(stress_xx[0:1], "gx", -1)
        prior_x = passed_along(jnp.stack([stress_xy[-1:], stress_xz[-1:]]), "gx", 1)
        next_y = passed_along(stress_yy[:, 0:1], "gy", -1)
        prior_y = passed_along(jnp.stack([stress_xy[:, -1:], stress_yz[:, -1:]]), "gy", 1)
        framed = [
            frame(stress_xx, next_x, None, None, None),
            frame(stress_yy, None, None, next_y, None),
            frame(stress_zz, None, None, None, None),
            frame(stress_xy, None, prior_x[0], None, prior_y[0]),
            frame(stress_xz, None, prior_x[1], None, None),
            frame(stress_yz, None, None, None, prior_y[1]),
        ]
        velocity = move_velocity(velocity, framed, buoyancy, 1, 0)
        speed_x, speed_y, speed_z = velocity
        vel_next_x = passed_along(jnp.stack([speed_y[0:1], speed_z[0:1]]), "gx", -1)
        vel_prior_x = passed_along(speed_x[-1:], "gx", 1)
        vel_next_y = passed_along(jnp.stack([speed_x[:, 0:1], speed_z[:, 0:1]]), "gy", -1)
        vel_prior_y = passed_along(speed_y[:, -1:], "gy", 1)
        moved = [
            frame(speed_x, None, vel_prior_x, vel_next_y[0], None),
            frame(speed_y, vel_next_x[0], None, None, vel_prior_y),
            frame(speed_z, vel_next_x[1], None, vel_next_y[1], None),
        ]
        strain = strains(moved, 1)
        stress = move_stress(stress, strain, lame_lambda, shear_mu)
        trace = strain[0] + strain[1] + strain[2]
        stored = [forward[6 * step + index] for index in range(6)]
        grad_lambda = grad_lambda + trace * (stored[0] + stored[1] + stored[2])
        grad_mu = grad_mu + 2.0 * (
            strain[0] * stored[0] + strain[1] * stored[1] + strain[2] * stored[2]
        )
        grad_mu = grad_mu + strain[3] * stored[3] + strain[4] * stored[4] + strain[5] * stored[5]
    return (jnp.stack(velocity + stress), jnp.stack([grad_lambda, grad_mu]))


def solution(mesh):
    return jax.shard_map(
        on_device,
        mesh=mesh,
        in_specs=(
            P(None, "gx", "gy", None),
            P("gx", "gy", None),
            P("gx", "gy", None),
            P("gx", "gy", None),
            P("gx", None, "gy", None, None),
            P("gx", None, "gy", None),
            P("gx", None),
        ),
        out_specs=(P(None, "gx", "gy", None), P(None, "gx", "gy", None)),
        check_vma=False,
    )
```

profile of v0, /device:TPU:1, one launch (start us, length us, event | category | flops | bytes accessed | tf_op | source)
XLA Modules:
  0.0 134.4 jit_solution(2305762378154470871)
XLA Ops:
  0.6 5.2 %all-to-all-start = ((s32[1,8,1,12,2048]{4,2,3,0,1:T(1,128)}), s32[1,8,1,12,2048]{4,2,3,0,1:T(1,128)S(1)}, u32[]{:S(2)}, u32[]{:S(2)}) async-start(s32[1,8,1,12,2048]{4,2,3,0,1:T(1,128)} %bitcast.138), calls=%async_computation | async-start | bytes 1572864 | tf_op jit(solution)/shard_map/all_to_all | solution.py:127
  6.7 1.9 %collective-permute-start = (f32[1,32,512]{2,1,0:T(8,128)S(1)}, f32[1,32,512]{2,1,0:T(8,128)S(1)}, u32[]{:S(2)}, u32[]{:S(2)}) collective-permute-start(f32[1,32,512]{2,1,0:T(8,128)S(1)} %slice_bitcast_fusion.20), channel_id=1, source_target_pairs={{4,0},{8,4},{12,8},{16,12},{20,16},{24,20},{28,24},{5,1},{9,5},{13... | collective-permute-start | bytes 196616 | tf_op jit(solution)/shard_map/ppermute | solution.py:15
  8.6 0.9 stack.110
  9.6 3.8 %collective-permute-start.2 = (f32[2,1,32,512]{3,2,1,0:T(8,128)S(1)}, f32[2,1,32,512]{3,2,1,0:T(8,128)S(1)}, u32[]{:S(2)}, u32[]{:S(2)}) collective-permute-start(f32[2,1,32,512]{3,2,1,0:T(8,128)S(1)} %stack.110), channel_id=1, source_target_pairs={{0,4},{4,8},{8,12},{12,16},{16,20},{20,24},{24,28},{1,5},{5,9},{9,... | collective-permute-start | bytes 393224 | tf_op jit(solution)/shard_map/ppermute | solution.py:15
  13.4 1.5 %slice_bitcast_fusion.1 = (f32[4,32,512]{2,1,0:T(8,128)S(1)}, f32[4,32,512]{2,1,0:T(8,128)S(1)}, f32[4,32,512]{2,1,0:T(8,128)S(1)}, f32[4,32,512]{2,1,0:T(8,128)...) fusion(f32[9,4,32,512]{3,2,1,0:T(8,128)} %param.7), kind=kLoop, calls=%fused_computation.226 | loop fusion | bytes 3145728 | tf_op jit(solution)/shard_map/squeeze | solution.py:133
  14.9 1.3 collective-permute-start.4
  16.2 4.0 %collective-permute-start.1 = (f32[2,4,1,512]{3,2,1,0:T(1,128)S(1)}, f32[2,4,1,512]{3,2,1,0:T(1,128)S(1)}, u32[]{:S(2)}, u32[]{:S(2)}) collective-permute-start(f32[2,4,1,512]{3,2,1,0:T(1,128)S(1)} %pad_maximum_fusion.68), channel_id=1, source_target_pairs={{0,1},{1,2},{2,3},{4,5},{5,6},{6,7},{8,9},{9,10},{10,11},{12,13},{... | collective-permute-start | bytes 49160 | tf_op jit(solution)/shard_map/ppermute | solution.py:15
  22.7 3.2 %collective-permute-start.5 = (f32[4,1,512]{2,1,0:T(1,128)S(1)}, f32[4,1,512]{2,1,0:T(1,128)S(1)}, u32[]{:S(2)}, u32[]{:S(2)}) collective-permute-start(f32[4,1,512]{2,1,0:T(1,128)S(1)} %slice.546), channel_id=1, source_target_pairs={{0,1},{1,2},{2,3},{4,5},{5,6},{6,7},{8,9},{9,10},{10,11},{12,13},{... | collective-permute-start | bytes 24584 | tf_op jit(solution)/shard_map/ppermute | solution.py:15
  25.9 1.3 collective-permute-start.7
  27.2 3.9 %collective-permute-start.3 = (f32[1,32,512]{2,1,0:T(8,128)S(1)}, f32[1,32,512]{2,1,0:T(8,128)S(1)}, u32[]{:S(2)}, u32[]{:S(2)}) collective-permute-start(f32[1,32,512]{2,1,0:T(8,128)S(1)} %slice.543), channel_id=1, source_target_pairs={{0,4},{4,8},{8,12},{12,16},{16,20},{20,24},{24,28},{1,5},{5,9},{9,... | collective-permute-start | bytes 196616 | tf_op jit(solution)/shard_map/ppermute | solution.py:15
  31.2 1.9 %collective-permute-start.6 = (f32[2,1,32,512]{3,2,1,0:T(8,128)S(1)}, f32[2,1,32,512]{3,2,1,0:T(8,128)S(1)}, u32[]{:S(2)}, u32[]{:S(2)}) collective-permute-start(f32[2,1,32,512]{3,2,1,0:T(8,128)S(1)} %pad_maximum_fusion.65), channel_id=1, source_target_pairs={{4,0},{8,4},{12,8},{16,12},{20,16},{24,20},{28,24},{5,1},{9,5},{13... | collective-permute-start | bytes 393224 | tf_op jit(solution)/shard_map/ppermute | solution.py:15
  33.2 4.3 %collective-permute-done.6 = f32[2,1,32,512]{3,2,1,0:T(8,128)S(1)} collective-permute-done((f32[2,1,32,512]{3,2,1,0:T(8,128)S(1)}, f32[2,1,32,512]{3,2,1,0:T(8,128)S(1)}, u32[]{:S(2)}, u32[]{:S(2)}) %collective-permute-start.6) | collective-permute-done | bytes 131104 | tf_op jit(solution)/shard_map/ppermute | solution.py:15
  39.4 1.3 collective-permute-start.11
  40.7 1.9 %collective-permute-start.8 = (f32[1,32,512]{2,1,0:T(8,128)S(1)}, f32[1,32,512]{2,1,0:T(8,128)S(1)}, u32[]{:S(2)}, u32[]{:S(2)}) collective-permute-start(f32[1,32,512]{2,1,0:T(8,128)S(1)} %slice.554), channel_id=1, source_target_pairs={{4,0},{8,4},{12,8},{16,12},{20,16},{24,20},{28,24},{5,1},{9,5},{13... | collective-permute-start | bytes 196616 | tf_op jit(solution)/shard_map/ppermute | solution.py:15
  42.7 4.9 %collective-permute-start.9 = (f32[2,4,1,512]{3,2,1,0:T(1,128)S(1)}, f32[2,4,1,512]{3,2,1,0:T(1,128)S(1)}, u32[]{:S(2)}, u32[]{:S(2)}) collective-permute-start(f32[2,4,1,512]{3,2,1,0:T(1,128)S(1)} %pad_maximum_fusion.70), channel_id=1, source_target_pairs={{0,1},{1,2},{2,3},{4,5},{5,6},{6,7},{8,9},{9,10},{10,11},{12,13},{... | collective-permute-start | bytes 49160 | tf_op jit(solution)/shard_map/ppermute | solution.py:15
  47.6 3.9 %collective-permute-start.10 = (f32[2,1,32,512]{3,2,1,0:T(8,128)S(1)}, f32[2,1,32,512]{3,2,1,0:T(8,128)S(1)}, u32[]{:S(2)}, u32[]{:S(2)}) collective-permute-start(f32[2,1,32,512]{3,2,1,0:T(8,128)S(1)} %pad_maximum_fusion.66), channel_id=1, source_target_pairs={{0,4},{4,8},{8,12},{12,16},{16,20},{20,24},{24,28},{1,5},{5,9},{9,... | collective-permute-start | bytes 393224 | tf_op jit(solution)/shard_map/ppermute | solution.py:15
  51.6 1.9 %collective-permute-done.10 = f32[2,1,32,512]{3,2,1,0:T(8,128)S(1)} collective-permute-done((f32[2,1,32,512]{3,2,1,0:T(8,128)S(1)}, f32[2,1,32,512]{3,2,1,0:T(8,128)S(1)}, u32[]{:S(2)}, u32[]{:S(2)}) %collective-permute-start.10) | collective-permute-done | bytes 131104 | tf_op jit(solution)/shard_map/ppermute | solution.py:15
  53.6 0.9 bitcast_dynamic-update-slice_fusion.8
  54.5 0.9 bitcast_dynamic-update-slice_fusion.7
  55.5 0.9 bitcast_dynamic-update-slice_fusion.6
  56.4 3.4 %collective-permute-start.13 = (f32[4,1,512]{2,1,0:T(1,128)S(1)}, f32[4,1,512]{2,1,0:T(1,128)S(1)}, u32[]{:S(2)}, u32[]{:S(2)}) collective-permute-start(f32[4,1,512]{2,1,0:T(1,128)S(1)} %slice.566), channel_id=1, source_target_pairs={{0,1},{1,2},{2,3},{4,5},{5,6},{6,7},{8,9},{9,10},{10,11},{12,13},{... | collective-permute-start | bytes 24584 | tf_op jit(solution)/shard_map/ppermute | solution.py:15
  59.8 1.3 collective-permute-start.15
  61.1 4.6 %collective-permute-start.12 = (f32[1,32,512]{2,1,0:T(8,128)S(1)}, f32[1,32,512]{2,1,0:T(8,128)S(1)}, u32[]{:S(2)}, u32[]{:S(2)}) collective-permute-start(f32[1,32,512]{2,1,0:T(8,128)S(1)} %slice.565), channel_id=1, source_target_pairs={{0,4},{4,8},{8,12},{12,16},{16,20},{20,24},{24,28},{1,5},{5,9},{9,... | collective-permute-start | bytes 196616 | tf_op jit(solution)/shard_map/ppermute | solution.py:15
  65.8 1.9 %collective-permute-start.14 = (f32[2,1,32,512]{3,2,1,0:T(8,128)S(1)}, f32[2,1,32,512]{3,2,1,0:T(8,128)S(1)}, u32[]{:S(2)}, u32[]{:S(2)}) collective-permute-start(f32[2,1,32,512]{3,2,1,0:T(8,128)S(1)} %pad_maximum_fusion.67), channel_id=1, source_target_pairs={{4,0},{8,4},{12,8},{16,12},{20,16},{24,20},{28,24},{5,1},{9,5},{13... | collective-permute-start | bytes 393224 | tf_op jit(solution)/shard_map/ppermute | solution.py:15
  67.8 5.0 %collective-permute-done.14 = f32[2,1,32,512]{3,2,1,0:T(8,128)S(1)} collective-permute-done((f32[2,1,32,512]{3,2,1,0:T(8,128)S(1)}, f32[2,1,32,512]{3,2,1,0:T(8,128)S(1)}, u32[]{:S(2)}, u32[]{:S(2)}) %collective-permute-start.14) | collective-permute-done | bytes 131104 | tf_op jit(solution)/shard_map/ppermute | solution.py:15
  73.5 1.2 pad_maximum_fusion
  74.7 6.4 %all-to-all-start.1 = ((f32[1,8,1,12]{3,2,0,1:T(1,128)}), f32[1,8,1,12]{3,2,0,1:T(1,128)}, u32[]{:S(2)}, u32[]{:S(2)}) async-start(f32[1,8,1,12]{3,2,0,1:T(1,128)} %bitcast.139), calls=%async_computation.1 | async-start | bytes 8192 | tf_op jit(solution)/shard_map/all_to_all | solution.py:128
  81.1 2.1 %fusion.2 = (s32[8,12,2048]{2,1,0:T(8,128)}, s32[8,12,2048]{2,1,0:T(8,128)}, s32[8,12,2048]{2,1,0:T(8,128)}) fusion(s32[1,8,1,12,2048]{4,2,3,0,1:T(1,128)S(1)} %all-to-all-done), kind=kLoop, calls=%fused_computation.40 | loop fusion | flops 1572864 | bytes 3145728 | tf_op jit(solution)/shard_map/sub | solution.py:19
  83.7 1.5 %copy.32 = s32[8,12,2048]{2,1,0:T(8,128)} copy(s32[8,12,2048]{2,0,1:T(8,128)S(1)} %fusion.9) | data formatting | bytes 1572864 | tf_op jit(solution)/shard_map/shift_right_arithmetic | solution.py:22
  85.2 4.8 %fusion = f32[8,12,8192]{2,1,0:T(8,128)} fusion(s32[8,12,2048]{2,1,0:T(8,128)} %copy.32, s32[8,12,2048]{2,1,0:T(8,128)} %get-tuple-element.37, s32[8,12,2048]{2,1,0:T(8,128)} %get-tuple-element.36, s32[8,12,2048]{2,1,0:T(8,128)} %get-tuple-element.35, f32[8,12]{1,0:T(8,128)} %bitcast.56), kind=kLoop, calls=%fused_computation.2 | loop fusion | flops 3932160 | bytes 6291840 | tf_op jit(solution)/shard_map/mul | solution.py:129
  90.0 5.1 %gather_fusion = f32[8,12,8192]{2,1,0:T(8,128)} fusion(f32[8,12,8192]{2,1,0:T(8,128)} %fusion, s32[1024]{0:T(1024)} %pad_clamp_fusion), kind=kCustom, calls=%fused_computation | custom fusion | bytes 6291488 | tf_op jit(solution)/shard_map/jit(_take)/gather | solution.py:130
  95.1 2.6 %select_bitcast_fusion = f32[12,8,8192]{2,0,1:T(8,128)S(1)} fusion(f32[8,12,8192]{2,1,0:T(8,128)} %gather_fusion, pred[8]{0:T(512)(128)(4,1)S(1)} %copy-done.50), kind=kLoop, calls=%fused_computation.3 | loop fusion | flops 786432 | bytes 6291464 | tf_op jit(solution)/shard_map/jit(_take)/select_n | solution.py:130
  97.7 9.6 %slice_reduce_fusion.11 = (f32[8,8192]{1,0:T(8,128)}, f32[8,8192]{1,0:T(8,128)}, f32[8,8192]{1,0:T(8,128)}, f32[8,8192]{1,0:T(8,128)S(1)}, f32[8,8192]{1,0:T(8,1...) fusion(f32[12,8,8192]{2,0,1:T(8,128)S(1)} %select_bitcast_fusion), kind=kLoop, calls=%fused_computation.171 | loop fusion | bytes 6291456 | tf_op jit(solution)/shard_map/slice | solution.py:164
  107.4 1.7 %squeeze.137 = f32[4,32,512]{2,1,0:T(8,128)} reshape(f32[8,8192]{1,0:T(8,128)} %get-tuple-element.2) | data formatting | bytes 524288 | tf_op jit(solution)/shard_map/squeeze | solution.py:164
  109.1 1.7 %squeeze.142 = f32[4,32,512]{2,1,0:T(8,128)} reshape(f32[8,8192]{1,0:T(8,128)} %get-tuple-element.9) | data formatting | bytes 524288 | tf_op jit(solution)/shard_map/squeeze | solution.py:164
  111.5 1.7 %squeeze.140 = f32[4,32,512]{2,1,0:T(8,128)} reshape(f32[8,8192]{1,0:T(8,128)} %get-tuple-element.11) | data formatting | bytes 524288 | tf_op jit(solution)/shard_map/squeeze | solution.py:164
  113.3 1.7 %squeeze.139 = f32[4,32,512]{2,1,0:T(8,128)} reshape(f32[8,8192]{1,0:T(8,128)} %get-tuple-element.12) | data formatting | bytes 524288 | tf_op jit(solution)/shard_map/squeeze | solution.py:164
  115.0 1.7 %squeeze.138 = f32[4,32,512]{2,1,0:T(8,128)} reshape(f32[8,8192]{1,0:T(8,128)} %get-tuple-element.13) | data formatting | bytes 524288 | tf_op jit(solution)/shard_map/squeeze | solution.py:164
  116.7 1.7 %squeeze.148 = f32[4,32,512]{2,1,0:T(8,128)} reshape(f32[8,8192]{1,0:T(8,128)} %get-tuple-element.3) | data formatting | bytes 524288 | tf_op jit(solution)/shard_map/squeeze | solution.py:164
  118.4 1.7 %squeeze.147 = f32[4,32,512]{2,1,0:T(8,128)} reshape(f32[8,8192]{1,0:T(8,128)} %get-tuple-element.4) | data formatting | bytes 524288 | tf_op jit(solution)/shard_map/squeeze | solution.py:164
  121.6 1.8 %squeeze.144 = f32[4,32,512]{2,1,0:T(8,128)} reshape(f32[8,8192]{1,0:T(8,128)} %get-tuple-element.7) | data formatting | bytes 524288 | tf_op jit(solution)/shard_map/squeeze | solution.py:164
  123.3 1.7 %squeeze.143 = f32[4,32,512]{2,1,0:T(8,128)} reshape(f32[8,8192]{1,0:T(8,128)} %get-tuple-element.8) | data formatting | bytes 524288 | tf_op jit(solution)/shard_map/squeeze | solution.py:164
  125.1 1.8 %add_bitcast_fusion.1 = (f32[1,4,32,512]{3,2,1,0:T(8,128)S(1)}, f32[4,32,512]{2,1,0:T(8,128)S(1)}) fusion(f32[4,32,512]{2,1,0:T(8,128)} %squeeze.142, f32[4,32,512]{2,1,0:T(8,128)} %squeeze.140, f32[4,32,512]{2,1,0:T(8,128)} %squeeze.141, f32[4,32,512]{2,1,0:T(8,128)} %copy-done.25, f32[4,32,512]{2,1,0:T(8,128)} %squeeze.139, f32[4,32,512]{2,1,0:T(8,128)} %squeeze.137, ...), kind=kLoop, calls=%fused_computation.216 | loop fusion | flops 1048576 | bytes 3772416 | tf_op jit(solution)/shard_map/stack | solution.py:170
  126.9 0.9 bitcast_dynamic-update-slice_fusion.5
  128.6 0.9 bitcast_dynamic-update-slice_fusion.3
  130.5 0.9 bitcast_dynamic-update-slice_fusion.1
  131.4 0.9 bitcast_dynamic-update-slice_fusion
  132.4 1.1 add_bitcast_fusion
  (188 shorter events, 11.4 us)
Async XLA Ops:
  0.6 19.6 %copy-start.51 = (s32[1,8]{1,0:T(1,128)S(1)}, s32[1,8]{1,0:T(1,128)}, u32[]{:S(2)}) copy-start(s32[1,8]{1,0:T(1,128)} %param.13) | copy-start | bytes 100
  0.6 74.0 %all-to-all-start = ((s32[1,8,1,12,2048]{4,2,3,0,1:T(1,128)}), s32[1,8,1,12,2048]{4,2,3,0,1:T(1,128)S(1)}, u32[]{:S(2)}, u32[]{:S(2)}) async-start(s32[1,8,1,12,2048]{4,2,3,0,1:T(1,128)} %bitcast.138), calls=%async_computation | async-start | bytes 1572864 | tf_op jit(solution)/shard_map/all_to_all | solution.py:127
  6.7 15.7 %collective-permute-start = (f32[1,32,512]{2,1,0:T(8,128)S(1)}, f32[1,32,512]{2,1,0:T(8,128)S(1)}, u32[]{:S(2)}, u32[]{:S(2)}) collective-permute-start(f32[1,32,512]{2,1,0:T(8,128)S(1)} %slice_bitcast_fusion.20), channel_id=1, source_target_pairs={{4,0},{8,4},{12,8},{16,12},{20,16},{24,20},{28,24},{5,1},{9,5},{13... | collective-permute-start | bytes 196616 | tf_op jit(solution)/shard_map/ppermute | solution.py:15
  9.5 12.4 %copy-start.1 = (f32[9,4,32,512]{3,2,1,0:T(8,128)S(1)}, f32[9,4,32,512]{3,2,1,0:T(8,128)}, u32[]{:S(2)}) copy-start(f32[9,4,32,512]{3,2,1,0:T(8,128)} %param.7) | copy-start | bytes 7077892
  9.6 12.4 %copy-start.2 = (f32[4,32,512]{2,1,0:T(8,128)S(1)}, f32[4,32,512]{2,1,0:T(8,128)}, u32[]{:S(2)}) copy-start(f32[4,32,512]{2,1,0:T(8,128)} %param.8) | copy-start | bytes 786436
  9.6 12.0 %collective-permute-start.2 = (f32[2,1,32,512]{3,2,1,0:T(8,128)S(1)}, f32[2,1,32,512]{3,2,1,0:T(8,128)S(1)}, u32[]{:S(2)}, u32[]{:S(2)}) collective-permute-start(f32[2,1,32,512]{3,2,1,0:T(8,128)S(1)} %stack.110), channel_id=1, source_target_pairs={{0,4},{4,8},{8,12},{12,16},{16,20},{20,24},{24,28},{1,5},{5,9},{9,... | collective-permute-start | bytes 393224 | tf_op jit(solution)/shard_map/ppermute | solution.py:15
  14.9 7.3 %collective-permute-start.4 = (f32[4,1,512]{2,1,0:T(1,128)S(1)}, f32[4,1,512]{2,1,0:T(1,128)S(1)}, u32[]{:S(2)}, u32[]{:S(2)}) collective-permute-start(f32[4,1,512]{2,1,0:T(1,128)S(1)} %slice.544), channel_id=1, source_target_pairs={{1,0},{2,1},{3,2},{5,4},{6,5},{7,6},{9,8},{10,9},{11,10},{13,12},{... | collective-permute-start | bytes 24584 | tf_op jit(solution)/shard_map/ppermute | solution.py:15
  16.2 5.4 %collective-permute-start.1 = (f32[2,4,1,512]{3,2,1,0:T(1,128)S(1)}, f32[2,4,1,512]{3,2,1,0:T(1,128)S(1)}, u32[]{:S(2)}, u32[]{:S(2)}) collective-permute-start(f32[2,4,1,512]{3,2,1,0:T(1,128)S(1)} %pad_maximum_fusion.68), channel_id=1, source_target_pairs={{0,1},{1,2},{2,3},{4,5},{5,6},{6,7},{8,9},{9,10},{10,11},{12,13},{... | collective-permute-start | bytes 49160 | tf_op jit(solution)/shard_map/ppermute | solution.py:15
  22.4 15.2 %copy-start = (f32[4,32,512]{2,1,0:T(8,128)S(1)}, f32[4,32,512]{2,1,0:T(8,128)}, u32[]{:S(2)}) copy-start(f32[4,32,512]{2,1,0:T(8,128)} %param.10) | copy-start | bytes 786436
  22.5 15.2 %copy-start.5 = (f32[4,32,512]{2,1,0:T(8,128)S(1)}, f32[4,32,512]{2,1,0:T(8,128)}, u32[]{:S(2)}) copy-start(f32[4,32,512]{2,1,0:T(8,128)} %param.9) | copy-start | bytes 786436
  22.7 10.4 %collective-permute-start.5 = (f32[4,1,512]{2,1,0:T(1,128)S(1)}, f32[4,1,512]{2,1,0:T(1,128)S(1)}, u32[]{:S(2)}, u32[]{:S(2)}) collective-permute-start(f32[4,1,512]{2,1,0:T(1,128)S(1)} %slice.546), channel_id=1, source_target_pairs={{0,1},{1,2},{2,3},{4,5},{5,6},{6,7},{8,9},{9,10},{10,11},{12,13},{... | collective-permute-start | bytes 24584 | tf_op jit(solution)/shard_map/ppermute | solution.py:15
  25.9 7.2 %collective-permute-start.7 = (f32[2,4,1,512]{3,2,1,0:T(1,128)S(1)}, f32[2,4,1,512]{3,2,1,0:T(1,128)S(1)}, u32[]{:S(2)}, u32[]{:S(2)}) collective-permute-start(f32[2,4,1,512]{3,2,1,0:T(1,128)S(1)} %pad_maximum_fusion.69), channel_id=1, source_target_pairs={{1,0},{2,1},{3,2},{5,4},{6,5},{7,6},{9,8},{10,9},{11,10},{13,12},{... | collective-permute-start | bytes 49160 | tf_op jit(solution)/shard_map/ppermute | solution.py:15
  27.2 10.3 %collective-permute-start.3 = (f32[1,32,512]{2,1,0:T(8,128)S(1)}, f32[1,32,512]{2,1,0:T(8,128)S(1)}, u32[]{:S(2)}, u32[]{:S(2)}) collective-permute-start(f32[1,32,512]{2,1,0:T(8,128)S(1)} %slice.543), channel_id=1, source_target_pairs={{0,4},{4,8},{8,12},{12,16},{16,20},{20,24},{24,28},{1,5},{5,9},{9,... | collective-permute-start | bytes 196616 | tf_op jit(solution)/shard_map/ppermute | solution.py:15
  31.2 6.3 %collective-permute-start.6 = (f32[2,1,32,512]{3,2,1,0:T(8,128)S(1)}, f32[2,1,32,512]{3,2,1,0:T(8,128)S(1)}, u32[]{:S(2)}, u32[]{:S(2)}) collective-permute-start(f32[2,1,32,512]{3,2,1,0:T(8,128)S(1)} %pad_maximum_fusion.65), channel_id=1, source_target_pairs={{4,0},{8,4},{12,8},{16,12},{20,16},{24,20},{28,24},{5,1},{9,5},{13... | collective-permute-start | bytes 393224 | tf_op jit(solution)/shard_map/ppermute | solution.py:15
  38.1 17.4 %copy-start.17 = (f32[4,32,512]{2,1,0:T(8,128)}, f32[4,32,512]{2,1,0:T(8,128)S(1)}, u32[]{:S(2)}) copy-start(f32[4,32,512]{2,1,0:T(8,128)S(1)} %get-tuple-element.18) | copy-start | bytes 786436
  38.9 15.7 %copy-start.7 = (f32[4,32,512]{2,1,0:T(8,128)}, f32[4,32,512]{2,1,0:T(8,128)S(1)}, u32[]{:S(2)}) copy-start(f32[4,32,512]{2,1,0:T(8,128)S(1)} %get-tuple-element.28) | copy-start | bytes 786436
  38.9 16.6 %copy-start.3 = (f32[4,32,512]{2,1,0:T(8,128)}, f32[4,32,512]{2,1,0:T(8,128)S(1)}, u32[]{:S(2)}) copy-start(f32[4,32,512]{2,1,0:T(8,128)S(1)} %get-tuple-element.27) | copy-start | bytes 786436
  39.4 15.1 %copy-start.19 = (f32[4,32,512]{2,1,0:T(8,128)}, f32[4,32,512]{2,1,0:T(8,128)S(1)}, u32[]{:S(2)}) copy-start(f32[4,32,512]{2,1,0:T(8,128)S(1)} %get-tuple-element.25) | copy-start | bytes 786436
  39.4 15.1 %copy-start.21 = (f32[4,32,512]{2,1,0:T(8,128)}, f32[4,32,512]{2,1,0:T(8,128)S(1)}, u32[]{:S(2)}) copy-start(f32[4,32,512]{2,1,0:T(8,128)S(1)} %get-tuple-element.24) | copy-start | bytes 786436
  39.4 15.1 %collective-permute-start.11 = (f32[4,1,512]{2,1,0:T(1,128)S(1)}, f32[4,1,512]{2,1,0:T(1,128)S(1)}, u32[]{:S(2)}, u32[]{:S(2)}) collective-permute-start(f32[4,1,512]{2,1,0:T(1,128)S(1)} %slice.563), channel_id=1, source_target_pairs={{1,0},{2,1},{3,2},{5,4},{6,5},{7,6},{9,8},{10,9},{11,10},{13,12},{... | collective-permute-start | bytes 24584 | tf_op jit(solution)/shard_map/ppermute | solution.py:15
  40.7 12.9 %collective-permute-start.8 = (f32[1,32,512]{2,1,0:T(8,128)S(1)}, f32[1,32,512]{2,1,0:T(8,128)S(1)}, u32[]{:S(2)}, u32[]{:S(2)}) collective-permute-start(f32[1,32,512]{2,1,0:T(8,128)S(1)} %slice.554), channel_id=1, source_target_pairs={{4,0},{8,4},{12,8},{16,12},{20,16},{24,20},{28,24},{5,1},{9,5},{13... | collective-permute-start | bytes 196616 | tf_op jit(solution)/shard_map/ppermute | solution.py:15
  42.7 8.9 %collective-permute-start.9 = (f32[2,4,1,512]{3,2,1,0:T(1,128)S(1)}, f32[2,4,1,512]{3,2,1,0:T(1,128)S(1)}, u32[]{:S(2)}, u32[]{:S(2)}) collective-permute-start(f32[2,4,1,512]{3,2,1,0:T(1,128)S(1)} %pad_maximum_fusion.70), channel_id=1, source_target_pairs={{0,1},{1,2},{2,3},{4,5},{5,6},{6,7},{8,9},{9,10},{10,11},{12,13},{... | collective-permute-start | bytes 49160 | tf_op jit(solution)/shard_map/ppermute | solution.py:15
  47.6 5.9 %collective-permute-start.10 = (f32[2,1,32,512]{3,2,1,0:T(8,128)S(1)}, f32[2,1,32,512]{3,2,1,0:T(8,128)S(1)}, u32[]{:S(2)}, u32[]{:S(2)}) collective-permute-start(f32[2,1,32,512]{3,2,1,0:T(8,128)S(1)} %pad_maximum_fusion.66), channel_id=1, source_target_pairs={{0,4},{4,8},{8,12},{12,16},{16,20},{20,24},{24,28},{1,5},{5,9},{9,... | collective-permute-start | bytes 393224 | tf_op jit(solution)/shard_map/ppermute | solution.py:15
  56.4 11.3 %collective-permute-start.13 = (f32[4,1,512]{2,1,0:T(1,128)S(1)}, f32[4,1,512]{2,1,0:T(1,128)S(1)}, u32[]{:S(2)}, u32[]{:S(2)}) collective-permute-start(f32[4,1,512]{2,1,0:T(1,128)S(1)} %slice.566), channel_id=1, source_target_pairs={{0,1},{1,2},{2,3},{4,5},{5,6},{6,7},{8,9},{9,10},{10,11},{12,13},{... | collective-permute-start | bytes 24584 | tf_op jit(solution)/shard_map/ppermute | solution.py:15
  59.8 7.9 %collective-permute-start.15 = (f32[2,4,1,512]{3,2,1,0:T(1,128)S(1)}, f32[2,4,1,512]{3,2,1,0:T(1,128)S(1)}, u32[]{:S(2)}, u32[]{:S(2)}) collective-permute-start(f32[2,4,1,512]{3,2,1,0:T(1,128)S(1)} %pad_maximum_fusion.71), channel_id=1, source_target_pairs={{1,0},{2,1},{3,2},{5,4},{6,5},{7,6},{9,8},{10,9},{11,10},{13,12},{... | collective-permute-start | bytes 49160 | tf_op jit(solution)/shard_map/ppermute | solution.py:15
  61.1 11.7 %collective-permute-start.12 = (f32[1,32,512]{2,1,0:T(8,128)S(1)}, f32[1,32,512]{2,1,0:T(8,128)S(1)}, u32[]{:S(2)}, u32[]{:S(2)}) collective-permute-start(f32[1,32,512]{2,1,0:T(8,128)S(1)} %slice.565), channel_id=1, source_target_pairs={{0,4},{4,8},{8,12},{12,16},{16,20},{20,24},{24,28},{1,5},{5,9},{9,... | collective-permute-start | bytes 196616 | tf_op jit(solution)/shard_map/ppermute | solution.py:15
  65.8 7.0 %collective-permute-start.14 = (f32[2,1,32,512]{3,2,1,0:T(8,128)S(1)}, f32[2,1,32,512]{3,2,1,0:T(8,128)S(1)}, u32[]{:S(2)}, u32[]{:S(2)}) collective-permute-start(f32[2,1,32,512]{3,2,1,0:T(8,128)S(1)} %pad_maximum_fusion.67), channel_id=1, source_target_pairs={{4,0},{8,4},{12,8},{16,12},{20,16},{24,20},{28,24},{5,1},{9,5},{13... | collective-permute-start | bytes 393224 | tf_op jit(solution)/shard_map/ppermute | solution.py:15
  67.8 5.0 %copy-start.46 = (f32[6,1,512]{2,1,0:T(1,128)}, f32[6,1,512]{2,1,0:T(1,128)S(1)}, u32[]{:S(2)}) copy-start(f32[6,1,512]{2,1,0:T(1,128)S(1)} %pad.131) | copy-start | bytes 36868
  67.8 5.0 %copy-start.48 = (f32[6,1,512]{2,1,0:T(1,128)}, f32[6,1,512]{2,1,0:T(1,128)S(1)}, u32[]{:S(2)}) copy-start(f32[6,1,512]{2,1,0:T(1,128)S(1)} %pad.129) | copy-start | bytes 36868
  74.7 10.5 %all-to-all-start.1 = ((f32[1,8,1,12]{3,2,0,1:T(1,128)}), f32[1,8,1,12]{3,2,0,1:T(1,128)}, u32[]{:S(2)}, u32[]{:S(2)}) async-start(f32[1,8,1,12]{3,2,0,1:T(1,128)} %bitcast.139), calls=%async_computation.1 | async-start | bytes 8192 | tf_op jit(solution)/shard_map/all_to_all | solution.py:128
  90.0 5.1 %copy-start.50 = (pred[8]{0:T(512)(128)(4,1)S(1)}, pred[8]{0:T(512)(128)(4,1)}, u32[]{:S(2)}) copy-start(pred[8]{0:T(512)(128)(4,1)} %compare_and_fusion) | copy-start | bytes 28
  111.5 13.5 %copy-start.24 = (f32[1,32,512]{2,1,0:T(8,128)S(1)}, f32[1,32,512]{2,1,0:T(8,128)}, u32[]{:S(2)}) copy-start(f32[1,32,512]{2,1,0:T(8,128)} %copy-done.23) | copy-start | bytes 196612
  111.5 13.5 %copy-start.33 = (f32[1,32,512]{2,1,0:T(8,128)S(1)}, f32[1,32,512]{2,1,0:T(8,128)}, u32[]{:S(2)}) copy-start(f32[1,32,512]{2,1,0:T(8,128)} %copy-done.32) | copy-start | bytes 196612
  121.6 5.3 %copy-start.6 = (f32[4,32,512]{2,1,0:T(8,128)S(1)}, f32[4,32,512]{2,1,0:T(8,128)}, u32[]{:S(2)}) copy-start(f32[4,32,512]{2,1,0:T(8,128)} %param.9) | copy-start | bytes 786436
  121.6 5.3 %copy-start.20 = (f32[4,32,512]{2,1,0:T(8,128)S(1)}, f32[4,32,512]{2,1,0:T(8,128)}, u32[]{:S(2)}) copy-start(f32[4,32,512]{2,1,0:T(8,128)} %copy-done.19) | copy-start | bytes 786436
  125.1 2.7 %copy-start.22 = (f32[4,32,512]{2,1,0:T(8,128)S(1)}, f32[4,32,512]{2,1,0:T(8,128)}, u32[]{:S(2)}) copy-start(f32[4,32,512]{2,1,0:T(8,128)} %copy-done.21) | copy-start | bytes 786436
  127.8 2.8 %copy-start.9 = (f32[6,34,512]{2,1,0:T(8,128)S(1)}, f32[6,34,512]{2,1,0:T(8,128)}, u32[]{:S(2)}) copy-start(f32[6,34,512]{2,1,0:T(8,128)} %get-tuple-element.48) | copy-start | bytes 1253380
  127.8 2.8 %copy-start.39 = (f32[1,32,512]{2,1,0:T(8,128)S(1)}, f32[1,32,512]{2,1,0:T(8,128)}, u32[]{:S(2)}) copy-start(f32[1,32,512]{2,1,0:T(8,128)} %copy-done.38) | copy-start | bytes 196612
  128.6 2.8 %copy-start.4 = (f32[4,32,512]{2,1,0:T(8,128)S(1)}, f32[4,32,512]{2,1,0:T(8,128)}, u32[]{:S(2)}) copy-start(f32[4,32,512]{2,1,0:T(8,128)} %copy-done.3) | copy-start | bytes 786436
  128.6 2.8 %copy-start.10 = (f32[6,34,512]{2,1,0:T(8,128)S(1)}, f32[6,34,512]{2,1,0:T(8,128)}, u32[]{:S(2)}) copy-start(f32[6,34,512]{2,1,0:T(8,128)} %get-tuple-element.46) | copy-start | bytes 1253380
  128.6 2.8 %copy-start.49 = (f32[6,1,512]{2,1,0:T(1,128)S(1)}, f32[6,1,512]{2,1,0:T(1,128)}, u32[]{:S(2)}) copy-start(f32[6,1,512]{2,1,0:T(1,128)} %copy-done.48) | copy-start | bytes 36868
  129.6 2.7 %copy-start.12 = (f32[6,34,512]{2,1,0:T(8,128)S(1)}, f32[6,34,512]{2,1,0:T(8,128)}, u32[]{:S(2)}) copy-start(f32[6,34,512]{2,1,0:T(8,128)} %copy-done.11) | copy-start | bytes 1253380
  129.6 2.7 %copy-start.14 = (f32[6,34,512]{2,1,0:T(8,128)S(1)}, f32[6,34,512]{2,1,0:T(8,128)}, u32[]{:S(2)}) copy-start(f32[6,34,512]{2,1,0:T(8,128)} %copy-done.13) | copy-start | bytes 1253380
  129.6 2.7 %copy-start.16 = (f32[6,34,512]{2,1,0:T(8,128)S(1)}, f32[6,34,512]{2,1,0:T(8,128)}, u32[]{:S(2)}) copy-start(f32[6,34,512]{2,1,0:T(8,128)} %copy-done.15) | copy-start | bytes 1253380
  129.6 2.7 %copy-start.26 = (f32[4,32,512]{2,1,0:T(8,128)S(1)}, f32[4,32,512]{2,1,0:T(8,128)}, u32[]{:S(2)}) copy-start(f32[4,32,512]{2,1,0:T(8,128)} %squeeze.137) | copy-start | bytes 786436
  129.6 2.7 %copy-start.27 = (f32[4,32,512]{2,1,0:T(8,128)S(1)}, f32[4,32,512]{2,1,0:T(8,128)}, u32[]{:S(2)}) copy-start(f32[4,32,512]{2,1,0:T(8,128)} %squeeze.142) | copy-start | bytes 786436
  129.6 2.7 %copy-start.28 = (f32[4,32,512]{2,1,0:T(8,128)S(1)}, f32[4,32,512]{2,1,0:T(8,128)}, u32[]{:S(2)}) copy-start(f32[4,32,512]{2,1,0:T(8,128)} %squeeze.141) | copy-start | bytes 786436
  129.6 2.7 %copy-start.29 = (f32[4,32,512]{2,1,0:T(8,128)S(1)}, f32[4,32,512]{2,1,0:T(8,128)}, u32[]{:S(2)}) copy-start(f32[4,32,512]{2,1,0:T(8,128)} %squeeze.140) | copy-start | bytes 786436
  (22 other events, 42.0 us)
where the time goes:
time: 137 us; the launch traced here: 134 us
  starting transfers between devices  56.2 us (41%)
  local copies, waits for them, and re-layouts  39.1 us (29%)
  other arithmetic  26.2 us (19%)
  waiting for transfers between devices  11.1 us (8%)
  between operations  1.76 us (1%)
    ppermute x16, starting transfers between devices, passed_along(): lax.ppermute(value, axis, [(source, source + steps) for source in range(f...  44.5 us
    squeeze x12, local copies, waits for them, and re-layouts, on_device(): stored = [forward[6 * step + index] for index in range(6)]  17.7 us
    ppermute x16, waiting for transfers between devices, passed_along(): lax.ppermute(value, axis, [(source, source + steps) for source in range(f...  11.1 us
    slice x1, local copies, waits for them, and re-layouts, on_device(): stored = [forward[6 * step + index] for index in range(6)]  9.63 us
    unnamed x8, other arithmetic  6.99 us
    all_to_all x1, starting transfers between devices, on_device(): lax.all_to_all(scales, 'gx', split_axis=1, concat_axis=0, tiled=True)  6.43 us
    all_to_all x1, starting transfers between devices, on_device(): lax.all_to_all(packed, 'gx', split_axis=1, concat_axis=0, tiled=True)  5.22 us
    gather x1, local copies, waits for them, and re-layouts, on_device(): ordered = jnp.take(blocks, inverse, axis=0)  5.12 us
  transfers between devices with their start and end apart: 18, of which 3 were waited for; matrix products, arithmetic and copies ran while one was open for 11% of the time, Pallas kernels for 0%

commit v1 on v0

v1 whole, which is shorter than its diff:
```python
import functools

import jax
import jax.numpy as jnp
from jax import lax
from jax.experimental import pallas as pl
from jax.experimental.pallas import tpu as pltpu
from jax.sharding import PartitionSpec as P

MESH = pl.DeviceIdType.MESH
STEPS = 2
COURANT = 0.15
ROWS = 8

VX, VY, VZ, SXX, SYY, SZZ, SXY, SXZ, SYZ = range(9)

STRESS_X = ((SXX, -1), (SXY, 1), (SXZ, 1))
STRESS_Y = ((SYY, -1), (SXY, 1), (SYZ, 1))
SPEED_X = ((VY, -1), (VZ, -1), (VX, 1))
SPEED_Y = ((VX, -1), (VZ, -1), (VY, 1))


def partner(me, distance, count):
    if count & (count - 1):
        return lax.rem(me + distance, count)
    result, bit = me, 1
    while bit < count:
        if distance & bit:
            result = result + bit - 2 * bit * ((me // bit) % 2)
        bit *= 2
    return result


def kernel(n_x, n_y, adj, buoy, lam, shear, packed, scales, perm, out, grads,
           cur, coef, strain, gsum, halo_x, halo_y, send_y, words, factors, factor_s, inv,
           in_sem, out_sem, xs_sem, xr_sem, ys_sem, yr_sem, ws_sem, wr_sem, fs_sem, fr_sem, loc_sem):
    cx, cy, cz = buoy.shape
    comp = packed.shape[1]
    lanes = packed.shape[3]
    segw = packed.shape[2] * lanes
    tiles = cy // ROWS
    me_x, me_y = lax.axis_index("gx"), lax.axis_index("gy")

    loads = []
    for index in (SXX, SXY, SXZ, SYY, SYZ, SZZ, VX, VY, VZ):
        loads.append(pltpu.make_async_copy(adj.at[index], cur.at[index, pl.ds(1, cx)], in_sem.at[index]))
    for index, ref in enumerate((buoy, lam, shear)):
        loads.append(pltpu.make_async_copy(ref, coef.at[index], in_sem.at[9 + index]))
    own_words = pltpu.make_async_copy(packed.at[me_x], words.at[me_x], loc_sem.at[0])
    own_factor = pltpu.make_async_copy(scales.at[0, me_x], factors.at[me_x], loc_sem.at[1])
    for copy in loads:
        copy.start()
    own_words.start()
    own_factor.start()

    barrier = pltpu.get_barrier_semaphore()
    for distance in range(1, n_x):
        pl.semaphore_signal(barrier, inc=1, device_id={"gx": partner(me_x, distance, n_x)}, device_id_type=MESH)

    def edge(way, axis):
        me, count = (me_x, n_x) if axis == "gx" else (me_y, n_y)
        return (me > 0) if way < 0 else (me < count - 1)

    for way in (-1, 1):
        @pl.when(edge(way, "gy"))
        def _():
            pl.semaphore_signal(barrier, inc=1, device_id={"gy": me_y + way}, device_id_type=MESH)

    pl.semaphore_wait(barrier, n_x - 1 + jnp.minimum(me_y, 1) + jnp.minimum(n_y - 1 - me_y, 1))

    def copy_x(step, kind, field, way, source):
        slot = 6 * step + kind
        return pltpu.make_async_remote_copy(
            src_ref=source, dst_ref=halo_x.at[slot], send_sem=xs_sem.at[slot], recv_sem=xr_sem.at[slot],
            device_id={"gx": me_x + way}, device_id_type=MESH)

    def copy_y(step, kind, way):
        slot = 6 * step + kind
        return pltpu.make_async_remote_copy(
            src_ref=send_y.at[slot], dst_ref=halo_y.at[slot], send_sem=ys_sem.at[slot], recv_sem=yr_sem.at[slot],
            device_id={"gy": me_y + way}, device_id_type=MESH)

    def layer(field, way):
        return cur.at[field, 1 if way < 0 else cx]

    def word_copy(distance):
        to = partner(me_x, distance, n_x)
        return pltpu.make_async_remote_copy(
            src_ref=packed.at[to], dst_ref=words.at[me_x], send_sem=ws_sem.at[distance],
            recv_sem=wr_sem.at[distance], device_id={"gx": to}, device_id_type=MESH)

    def factor_copy(distance):
        to = partner(me_x, distance, n_x)
        return pltpu.make_async_remote_copy(
            src_ref=scales.at[0, to], dst_ref=factors.at[me_x], send_sem=fs_sem.at[distance],
            recv_sem=fr_sem.at[distance], device_id={"gx": to}, device_id_type=MESH)

    def send_x(step, base, kinds, source, ways):
        for offset, (field, way) in enumerate(kinds):
            if way in ways:
                @pl.when(edge(way, "gx"))
                def _():
                    copy_x(step, base + offset, field, way, source(field, way)).start()

    def pack_rows(step, base, kinds):
        for offset, (field, way) in enumerate(kinds):
            row = 0 if way < 0 else cy - 1
            for x in range(cx):
                send_y[6 * step + base + offset, pl.ds(x, 1), :] = cur[field, 1 + x, pl.ds(row, 1), :]

    def send_rows(step, base, kinds):
        pack_rows(step, base, kinds)
        for offset, (field, way) in enumerate(kinds):
            @pl.when(edge(way, "gy"))
            def _():
                copy_y(step, base + offset, way).start()

    def finish_sends(step, base, kinds_x, kinds_y):
        for offset, (field, way) in enumerate(kinds_x):
            @pl.when(edge(way, "gx"))
            def _():
                copy_x(step, base + offset, field, way, layer(field, way)).wait_send()
        for offset, (field, way) in enumerate(kinds_y):
            @pl.when(edge(way, "gy"))
            def _():
                copy_y(step, base + offset, way).wait_send()

    def receive(step, base, kinds_x, kinds_y):
        for offset, (field, way) in enumerate(kinds_y):
            slot = 6 * step + base + offset

            @pl.when(edge(-way, "gy"))
            def _():
                copy_y(step, base + offset, way).wait_recv()

            @pl.when(jnp.logical_not(edge(-way, "gy")))
            def _():
                halo_y[slot] = jnp.zeros((cx, cz), jnp.float32)
        for offset, (field, way) in enumerate(kinds_x):
            slot = 6 * step + base + offset
            place = cx + 1 if way < 0 else 0

            @pl.when(edge(-way, "gx"))
            def _():
                copy_x(step, base + offset, field, way, layer(field, way)).wait_recv()
                cur[field, place] = halo_x[slot]

            @pl.when(jnp.logical_not(edge(-way, "gx")))
            def _():
                cur[field, place] = jnp.zeros((cy, cz), jnp.float32)

    groups = [[], [], [], []]
    half = max(n_x // 2, 1)
    for distance in range(1, n_x):
        if distance >= half:
            where = 0 if n_x < 8 else (1 if distance == half else 2 + (distance % 2))
        else:
            where = distance % 2
        if n_x == 8:
            where = {1: 0, 2: 0, 4: 0, 3: 1, 5: 1, 6: 2, 7: 3}[distance]
        groups[where].append(distance)

    def send_group(which):
        for distance in groups[which]:
            factor_copy(distance).start()
            word_copy(distance).start()

    sub = lax.broadcasted_iota(jnp.int32, (ROWS, cz), 0)
    lane = lax.broadcasted_iota(jnp.int32, (ROWS, cz), 1)
    first_row, last_row = sub == 0, sub == ROWS - 1
    first_lane, last_lane = lane == 0, lane == cz - 1

    def tile(field, x, t):
        return cur[field, x + 1, pl.ds(t * ROWS, ROWS), :]

    def z_before(value):
        return jnp.where(first_lane, 0.0, pltpu.roll(value, 1, 1))

    def z_after(value):
        return jnp.where(last_lane, 0.0, pltpu.roll(value, cz - 1, 1))

    def y_before(value, field, x, t, slot):
        row = halo_y[slot, pl.ds(x, 1), :] if t == 0 else cur[field, x + 1, pl.ds(t * ROWS - 1, 1), :]
        return jnp.where(first_row, jnp.broadcast_to(row, value.shape), pltpu.roll(value, 1, 0))

    def y_after(value, field, x, t, slot):
        row = halo_y[slot, pl.ds(x, 1), :] if t == tiles - 1 else cur[field, x + 1, pl.ds(t * ROWS + ROWS, 1), :]
        return jnp.where(last_row, jnp.broadcast_to(row, value.shape), pltpu.roll(value, ROWS - 1, 0))

    def velocity(step, x):
        slot = 6 * step
        for t in range(tiles):
            rows = pl.ds(t * ROWS, ROWS)
            scaled = COURANT * coef[0, x, rows, :]
            sxy, sxz, syz = tile(SXY, x, t), tile(SXZ, x, t), tile(SYZ, x, t)
            sxx, syy, szz = tile(SXX, x, t), tile(SYY, x, t), tile(SZZ, x, t)
            cur[VX, x + 1, rows, :] = tile(VX, x, t) - scaled * (
                (tile(SXX, x + 1, t) - sxx) + (sxy - y_before(sxy, SXY, x, t, slot + 1)) + (sxz - z_before(sxz)))
            cur[VY, x + 1, rows, :] = tile(VY, x, t) - scaled * (
                (sxy - tile(SXY, x - 1, t)) + (y_after(syy, SYY, x, t, slot) - syy) + (syz - z_before(syz)))
            cur[VZ, x + 1, rows, :] = tile(VZ, x, t) - scaled * (
                (sxz - tile(SXZ, x - 1, t)) + (syz - y_before(syz, SYZ, x, t, slot + 2)) + (z_after(szz) - szz))

    def stress(step, x):
        slot = 6 * step + 3
        for t in range(tiles):
            rows = pl.ds(t * ROWS, ROWS)
            vx, vy, vz = tile(VX, x, t), tile(VY, x, t), tile(VZ, x, t)
            exx = vx - tile(VX, x - 1, t)
            eyy = vy - y_before(vy, VY, x, t, slot + 2)
            ezz = vz - z_before(vz)
            exy = (y_after(vx, VX, x, t, slot) - vx) + (tile(VY, x + 1, t) - vy)
            exz = (z_after(vx) - vx) + (tile(VZ, x + 1, t) - vz)
            eyz = (z_after(vy) - vy) + (y_after(vz, VZ, x, t, slot + 1) - vz)
            both = (exx, eyy, ezz, exy, exz, eyz)
            for index, value in enumerate(both):
                strain[6 * step + index, x, rows, :] = value
            pull = (COURANT * coef[1, x, rows, :]) * (exx + eyy + ezz)
            mu = COURANT * coef[2, x, rows, :]
            for index in range(3):
                cur[SXX + index, x + 1, rows, :] = tile(SXX + index, x, t) - (pull + (2.0 * mu) * both[index])
            for index in range(3, 6):
                cur[SXX + index, x + 1, rows, :] = tile(SXX + index, x, t) - mu * both[index]

    def over(first, last, body):
        def run(x, carry):
            body(x)
            return carry
        lax.fori_loop(first, last, run, 0)

    def ends(body):
        def run(index, carry):
            body(index * (cx - 1))
            return carry
        lax.fori_loop(0, 2, run, 0)

    for step in range(STEPS):
        if step == 0:
            send_x(0, 0, STRESS_X, lambda field, way: adj.at[field, 0 if way < 0 else cx - 1], (-1, 1))
            for copy in loads:
                copy.wait()
            send_rows(0, 0, STRESS_Y)
            send_group(0)
            def invert(block, carry):
                total = jnp.int32(0)
                for holder in range(n_x):
                    total = jnp.where(perm[0, holder] == block, holder, total)
                inv[block] = total
                return carry
            lax.fori_loop(0, n_x, invert, 0)
        receive(step, 0, STRESS_X, STRESS_Y)
        if step > 0:
            finish_sends(step - 1, 3, SPEED_X, SPEED_Y)
        ends(functools.partial(velocity, step))
        send_x(step, 3, SPEED_X, layer, (-1, 1))
        over(1, cx - 1, functools.partial(velocity, step))
        send_rows(step, 3, SPEED_Y)
        send_group(1 + 2 * step)
        if step == STEPS - 1:
            speed_out = [pltpu.make_async_copy(cur.at[f, pl.ds(1, cx)], out.at[f], out_sem.at[f]) for f in range(3)]
            for copy in speed_out:
                copy.start()
        receive(step, 3, SPEED_X, SPEED_Y)
        finish_sends(step, 0, STRESS_X, STRESS_Y)
        ends(functools.partial(stress, step))
        if step < STEPS - 1:
            send_x(step + 1, 0, STRESS_X, layer, (-1, 1))
        over(1, cx - 1, functools.partial(stress, step))
        if step < STEPS - 1:
            send_rows(step + 1, 0, STRESS_Y)
            send_group(2 + 2 * step)
    finish_sends(STEPS - 1, 3, SPEED_X, SPEED_Y)
    stress_out = [pltpu.make_async_copy(cur.at[f, pl.ds(1, cx)], out.at[f], out_sem.at[f]) for f in range(3, 9)]
    for copy in stress_out:
        copy.start()

    own_words.wait()
    own_factor.wait()
    for distance in range(1, n_x):
        factor_copy(distance).wait()
    to_scalar = pltpu.make_async_copy(factors, factor_s, loc_sem.at[2])
    to_scalar.start()
    for distance in range(1, n_x):
        word_copy(distance).wait()
    to_scalar.wait()

    width = lanes
    per_x = cy * cz // (4 * segw)

    def source(row, chunk):
        offset = row * cz + chunk * width
        within = offset % (4 * segw)
        return offset // (4 * segw), within % segw, within // segw

    sub_w = lax.broadcasted_iota(jnp.int32, (ROWS, width), 0)

    def gradient(x):
        made = {}
        for t in range(tiles):
            for chunk in range(cz // width):
                rows = pl.ds(t * ROWS, ROWS)
                columns = pl.ds(chunk * width, width)
                plan = [source(t * ROWS + r, chunk) for r in range(ROWS)]
                shift = jnp.full((ROWS, width), 8 * plan[0][2], jnp.int32)
                for r in range(1, ROWS):
                    if plan[r][2] != plan[r - 1][2]:
                        shift = jnp.where(sub_w >= r, 8 * plan[r][2], shift)
                key = tuple(p[:2] for p in plan)
                distinct = list(dict.fromkeys(key))
                masks = []
                for item in distinct[1:]:
                    mask = None
                    for r in range(ROWS):
                        if key[r] == item:
                            mask = (sub_w == r) if mask is None else mask | (sub_w == r)
                    masks.append(mask)
                holders = {b: inv[x * per_x + b] for b in dict.fromkeys(k[0] for k in key)}
                blocks = [k[0] for k in key]

                def stored(c):
                    if (key, c) not in made:
                        word = None
                        for position, (block, start) in enumerate(distinct):
                            piece = jnp.broadcast_to(
                                words[holders[block], c, pl.ds(start // lanes, 1), :], (ROWS, width))
                            word = piece if word is None else jnp.where(masks[position - 1], piece, word)
                        made[key, c] = word ^ jnp.int32(-2147483648)
                    byte = (lax.shift_right_logical(made[key, c], shift) & 255) - 128
                    factor = None
                    for r in range(ROWS):
                        if r == 0:
                            factor = factor_s[holders[blocks[0]], 0, c]
                        elif blocks[r] != blocks[r - 1]:
                            factor = jnp.where(sub_w >= r, factor_s[holders[blocks[r]], 0, c], factor)
                    return byte.astype(jnp.float32) * factor

                grad_lambda = jnp.zeros((ROWS, width), jnp.float32)
                grad_mu = jnp.zeros((ROWS, width), jnp.float32)
                for step in range(comp // 6):
                    e = [strain[6 * step + index, x, rows, columns] for index in range(6)]
                    f = [stored(6 * step + index) for index in range(6)]
                    grad_lambda = grad_lambda + (e[0] + e[1] + e[2]) * (f[0] + f[1] + f[2])
                    grad_mu = grad_mu + 2.0 * (e[0] * f[0] + e[1] * f[1] + e[2] * f[2])
                    grad_mu = grad_mu + e[3] * f[3] + e[4] * f[4] + e[5] * f[5]
                gsum[0, x, rows, columns] = grad_lambda
                gsum[1, x, rows, columns] = grad_mu

    over(0, cx, gradient)
    grad_out = pltpu.make_async_copy(gsum, grads, loc_sem.at[3])
    grad_out.start()
    for copy in speed_out + stress_out:
        copy.wait()
    grad_out.wait()


def on_device(n_x, n_y, adjoint, buoyancy, lame_lambda, shear_mu, packed, scales, perm):
    fields, cx, cy, cz = adjoint.shape
    comp, segw = packed.shape[3:]
    lanes = min(128, segw)
    packed = packed.reshape(n_x, comp, segw // lanes, lanes)
    halos = 6 * STEPS
    dma = pltpu.SemaphoreType.DMA
    any_space = pl.BlockSpec(memory_space=pl.ANY)
    return pl.pallas_call(
        functools.partial(kernel, n_x, n_y),
        out_shape=(jax.ShapeDtypeStruct(adjoint.shape, jnp.float32),
                   jax.ShapeDtypeStruct((2, cx, cy, cz), jnp.float32)),
        in_specs=[pl.BlockSpec(memory_space=pltpu.HBM)] * 6 + [pl.BlockSpec(memory_space=pltpu.SMEM)],
        out_specs=(any_space, any_space),
        scratch_shapes=[
            pltpu.VMEM((fields, cx + 2, cy, cz), jnp.float32),
            pltpu.VMEM((3, cx, cy, cz), jnp.float32),
            pltpu.VMEM((comp, cx, cy, cz), jnp.float32),
            pltpu.VMEM((2, cx, cy, cz), jnp.float32),
            pltpu.VMEM((halos, cy, cz), jnp.float32),
            pltpu.VMEM((halos, cx, cz), jnp.float32),
            pltpu.VMEM((halos, cx, cz), jnp.float32),
            pltpu.VMEM((n_x, comp, segw // lanes, lanes), jnp.int32),
            pltpu.VMEM((n_x, 1, comp), jnp.float32),
            pltpu.SMEM((n_x, 1, comp), jnp.float32),
            pltpu.SMEM((n_x,), jnp.int32),
            dma((12,)), dma((9,)), dma((halos,)), dma((halos,)), dma((halos,)), dma((halos,)),
            dma((n_x,)), dma((n_x,)), dma((n_x,)), dma((n_x,)), dma((4,)),
        ],
        compiler_params=pltpu.CompilerParams(collective_id=0, has_side_effects=True,
                                             vmem_limit_bytes=40 * 1024 * 1024),
    )(adjoint, buoyancy, lame_lambda, shear_mu, packed, scales, perm)


def solution(mesh):
    return jax.shard_map(
        functools.partial(on_device, mesh.shape["gx"], mesh.shape["gy"]),
        mesh=mesh,
        in_specs=(
            P(None, "gx", "gy", None),
            P("gx", "gy", None),
            P("gx", "gy", None),
            P("gx", "gy", None),
            P("gx", None, "gy", None, None),
            P("gx", None, "gy", None),
            P("gx", None),
        ),
        out_specs=(P(None, "gx", "gy", None), P(None, "gx", "gy", None)),
        check_vma=False,
    )
```

time: 137 us -> 36.1 us (0.26); the launches traced: 134 us -> 35.8 us
  starting transfers between devices: 56.2 us -> 0 us
  local copies, waits for them, and re-layouts: 39.1 us -> 9.18 us
  other arithmetic: 26.2 us -> 0 us
  Pallas kernels: 0 us -> 26 us
  waiting for transfers between devices: 11.1 us -> 0 us
    ppermute x16 -> x0, starting transfers between devices: 44.5 us -> none  [passed_along(): lax.ppermute(value, axis, [(source, source + steps) for source in range(f...]
    pallas_call x0 -> x1, Pallas kernels: none -> 26 us  [on_device(): pl.pallas_call(functools.partial(kernel, n_x, n_y), out_shape=(jax.ShapeD...]
    squeeze x21 -> x0, local copies, waits for them, and re-layouts: 19.2 us -> none  [the longest x12 17.7 us: on_device(): stored = [forward[6 * step + index] for index in range(6)]]
    all_to_all x2 -> x0, starting transfers between devices: 11.7 us -> none  [the longest x1 6.43 us: on_device(): lax.all_to_all(scales, 'gx', split_axis=1, concat_axis=0, tiled=True)]
    ppermute x16 -> x0, waiting for transfers between devices: 11.1 us -> none  [passed_along(): lax.ppermute(value, axis, [(source, source + steps) for source in range(f...]
    slice x9 -> x0, local copies, waits for them, and re-layouts: 10.5 us -> none  [the longest x1 9.63 us: on_device(): stored = [forward[6 * step + index] for index in range(6)]]
    unnamed x104 -> x16, local copies, waits for them, and re-layouts: 1.48 us -> 9.18 us
    unnamed x8 -> x0, other arithmetic: 6.99 us -> none
  transfers between devices with their start and end apart: 18 -> 0, of which waited for: 3 -> 0; matrix products, arithmetic and copies ran while one was open for 11% -> 0% of each run, Pallas kernels for 0% -> 0%
where the time goes in v1:
time: 36.1 us; the launch traced here: 35.8 us
  Pallas kernels  26 us (72%)
  local copies, waits for them, and re-layouts  9.18 us (25%)
  between operations  0.66 us (2%)
    pallas_call x1, Pallas kernels, on_device(): pl.pallas_call(functools.partial(kernel, n_x, n_y), out_shape=(jax.ShapeD...  26 us
    unnamed x16, local copies, waits for them, and re-layouts  9.18 us

profile of v1, /device:TPU:1, one launch (start us, length us, event | category | flops | bytes accessed | tf_op | source)
XLA Modules:
  0.0 35.8 jit_solution(15762663441686357357)
XLA Ops:
  0.6 0.0 copy-start
  0.6 1.7 %copy-done = f32[9,4,32,512]{3,2,1,0:T(8,128)S(1)} copy-done((f32[9,4,32,512]{3,2,1,0:T(8,128)S(1)}, f32[9,4,32,512]{3,2,1,0:T(8,128)}, u32[]{:S(2)}) %copy-start) | copy-done | bytes 2359320
  2.3 0.0 copy-start.1
  2.3 1.1 %copy-done.1 = s32[1,8,1,12,2048]{4,2,3,1,0:T(1,128)S(1)} copy-done((s32[1,8,1,12,2048]{4,2,3,1,0:T(1,128)S(1)}, s32[1,8,1,12,2048]{4,2,3,1,0:T(1,128)}, u32[]{:S(2)}) %copy-start.1) | copy-done | bytes 786456
  3.4 0.0 copy-start.2
  3.4 0.9 %copy-done.2 = f32[4,32,512]{2,1,0:T(8,128)S(1)} copy-done((f32[4,32,512]{2,1,0:T(8,128)S(1)}, f32[4,32,512]{2,1,0:T(8,128)}, u32[]{:S(2)}) %copy-start.2) | copy-done | bytes 262168
  4.4 0.0 copy-start.3
  4.4 0.9 %copy-done.3 = f32[4,32,512]{2,1,0:T(8,128)S(1)} copy-done((f32[4,32,512]{2,1,0:T(8,128)S(1)}, f32[4,32,512]{2,1,0:T(8,128)}, u32[]{:S(2)}) %copy-start.3) | copy-done | bytes 262168
  5.3 0.0 copy-start.4
  5.3 0.9 %copy-done.4 = f32[4,32,512]{2,1,0:T(8,128)S(1)} copy-done((f32[4,32,512]{2,1,0:T(8,128)S(1)}, f32[4,32,512]{2,1,0:T(8,128)}, u32[]{:S(2)}) %copy-start.4) | copy-done | bytes 262168
  6.3 0.0 copy-start.5
  6.3 0.7 %copy-done.5 = f32[1,8,1,12]{3,2,1,0:T(1,128)S(1)} copy-done((f32[1,8,1,12]{3,2,1,0:T(1,128)S(1)}, f32[1,8,1,12]{3,2,1,0:T(1,128)}, u32[]{:S(2)}) %copy-start.5) | copy-done | bytes 408
  7.0 0.0 copy-start.6
  7.0 0.7 %copy-done.6 = s32[1,8]{1,0:T(1,128)S(1)} copy-done((s32[1,8]{1,0:T(1,128)S(1)}, s32[1,8]{1,0:T(1,128)}, u32[]{:S(2)}) %copy-start.6) | copy-done | bytes 56
  7.6 26.0 %shard_map.86 = (f32[9,4,32,512]{3,2,1,0:T(8,128)S(1)}, f32[2,4,32,512]{3,2,1,0:T(8,128)S(1)}) custom-call(f32[9,4,32,512]{3,2,1,0:T(8,128)S(1)} %copy-done, f32[4,32,512]{2,1,0:T(8,128)S(1)} %copy-done.2, f32[4,32,512]{2,1,0:T(8,128)S(1)} %copy-done.3, f32[4,32,512]{2,1,0:T(8,128)S(1)} %copy-done.4, s32[8,12,16,128]{3,2,1,0:T(8,128)S(1)} %bitcast.1, ...), custom_call_target="tpu_custom_call" | custom-call | tf_op jit(solution)/shard_map/pallas_call | solution.py:364
  33.6 1.4 %copy.11 = f32[9,4,32,512]{3,2,1,0:T(8,128)} copy(f32[9,4,32,512]{3,2,1,0:T(8,128)S(1)} %get-tuple-element.4) | data formatting | bytes 4718592
  35.0 0.8 %copy.12 = f32[2,4,32,512]{3,2,1,0:T(8,128)} copy(f32[2,4,32,512]{3,2,1,0:T(8,128)S(1)} %get-tuple-element.5) | data formatting | bytes 1048576
Async XLA Ops:
  0.6 1.7 %copy-start = (f32[9,4,32,512]{3,2,1,0:T(8,128)S(1)}, f32[9,4,32,512]{3,2,1,0:T(8,128)}, u32[]{:S(2)}) copy-start(f32[9,4,32,512]{3,2,1,0:T(8,128)} %adj.1) | copy-start | bytes 7077892
  2.3 1.1 %copy-start.1 = (s32[1,8,1,12,2048]{4,2,3,1,0:T(1,128)S(1)}, s32[1,8,1,12,2048]{4,2,3,1,0:T(1,128)}, u32[]{:S(2)}) copy-start(s32[1,8,1,12,2048]{4,2,3,1,0:T(1,128)} %param.11) | copy-start | bytes 2359300
  3.4 0.9 %copy-start.2 = (f32[4,32,512]{2,1,0:T(8,128)S(1)}, f32[4,32,512]{2,1,0:T(8,128)}, u32[]{:S(2)}) copy-start(f32[4,32,512]{2,1,0:T(8,128)} %buoy.1) | copy-start | bytes 786436
  4.4 0.9 %copy-start.3 = (f32[4,32,512]{2,1,0:T(8,128)S(1)}, f32[4,32,512]{2,1,0:T(8,128)}, u32[]{:S(2)}) copy-start(f32[4,32,512]{2,1,0:T(8,128)} %lam.1) | copy-start | bytes 786436
  5.3 0.9 %copy-start.4 = (f32[4,32,512]{2,1,0:T(8,128)S(1)}, f32[4,32,512]{2,1,0:T(8,128)}, u32[]{:S(2)}) copy-start(f32[4,32,512]{2,1,0:T(8,128)} %shear.1) | copy-start | bytes 786436
  6.3 0.7 %copy-start.5 = (f32[1,8,1,12]{3,2,1,0:T(1,128)S(1)}, f32[1,8,1,12]{3,2,1,0:T(1,128)}, u32[]{:S(2)}) copy-start(f32[1,8,1,12]{3,2,1,0:T(1,128)} %scales.1) | copy-start | bytes 1156
  7.0 0.7 %copy-start.6 = (s32[1,8]{1,0:T(1,128)S(1)}, s32[1,8]{1,0:T(1,128)}, u32[]{:S(2)}) copy-start(s32[1,8]{1,0:T(1,128)} %perm.1) | copy-start | bytes 100

commit v2 on v1

--- a/solution.py
+++ b/solution.py
@@ -14,10 +14,10 @@
 
 VX, VY, VZ, SXX, SYY, SZZ, SXY, SXZ, SYZ = range(9)
 
-STRESS_X = ((SXX, -1), (SXY, 1), (SXZ, 1))
-STRESS_Y = ((SYY, -1), (SXY, 1), (SYZ, 1))
-SPEED_X = ((VY, -1), (VZ, -1), (VX, 1))
-SPEED_Y = ((VX, -1), (VZ, -1), (VY, 1))
+STRESS_X = ((0, (SXX,), -1), (1, (SXY, SXZ), 1))
+STRESS_Y = ((0, (SYY,), -1), (1, (SXY, SYZ), 1))
+SPEED_X = ((3, (VY, VZ), -1), (5, (VX,), 1))
+SPEED_Y = ((3, (VX, VZ), -1), (5, (VY,), 1))
 
 
 def partner(me, distance, count):
@@ -32,8 +32,8 @@
 
 
 def kernel(n_x, n_y, adj, buoy, lam, shear, packed, scales, perm, out, grads,
-           cur, coef, strain, gsum, halo_x, halo_y, send_y, words, factors, factor_s, inv,
-           in_sem, out_sem, xs_sem, xr_sem, ys_sem, yr_sem, ws_sem, wr_sem, fs_sem, fr_sem, loc_sem):
+           cur, coef, strain, halo_x, halo_y, send_y, words, factors, factor_s, inv,
+           in_sem, xs_sem, xr_sem, ys_sem, yr_sem, ws_sem, wr_sem, fs_sem, fr_sem, loc_sem):
     cx, cy, cz = buoy.shape
     comp = packed.shape[1]
     lanes = packed.shape[3]
@@ -68,20 +68,27 @@
 
     pl.semaphore_wait(barrier, n_x - 1 + jnp.minimum(me_y, 1) + jnp.minimum(n_y - 1 - me_y, 1))
 
-    def copy_x(step, kind, field, way, source):
-        slot = 6 * step + kind
+    def copy_x(step, message, source):
+        start, fields, way = message
+        slot = 6 * step + start
         return pltpu.make_async_remote_copy(
-            src_ref=source, dst_ref=halo_x.at[slot], send_sem=xs_sem.at[slot], recv_sem=xr_sem.at[slot],
+            src_ref=source(fields, way), dst_ref=halo_x.at[pl.ds(slot, len(fields))],
+            send_sem=xs_sem.at[slot], recv_sem=xr_sem.at[slot],
             device_id={"gx": me_x + way}, device_id_type=MESH)
 
-    def copy_y(step, kind, way):
-        slot = 6 * step + kind
+    def copy_y(step, message):
+        start, fields, way = message
+        slot = 6 * step + start
         return pltpu.make_async_remote_copy(
-            src_ref=send_y.at[slot], dst_ref=halo_y.at[slot], send_sem=ys_sem.at[slot], recv_sem=yr_sem.at[slot],
+            src_ref=send_y.at[pl.ds(slot, len(fields))], dst_ref=halo_y.at[pl.ds(slot, len(fields))],
+            send_sem=ys_sem.at[slot], recv_sem=yr_sem.at[slot],
             device_id={"gy": me_y + way}, device_id_type=MESH)
 
-    def layer(field, way):
-        return cur.at[field, 1 if way < 0 else cx]
+    def layer(fields, way):
+        return cur.at[pl.ds(fields[0], len(fields)), 1 if way < 0 else cx]
+
+    def first_layer(fields, way):
+        return adj.at[pl.ds(fields[0], len(fields)), 0 if way < 0 else cx - 1]
 
     def word_copy(distance):
         to = partner(me_x, distance, n_x)
@@ -95,59 +102,60 @@
             src_ref=scales.at[0, to], dst_ref=factors.at[me_x], send_sem=fs_sem.at[distance],
             recv_sem=fr_sem.at[distance], device_id={"gx": to}, device_id_type=MESH)
 
-    def send_x(step, base, kinds, source, ways):
-        for offset, (field, way) in enumerate(kinds):
-            if way in ways:
-                @pl.when(edge(way, "gx"))
-                def _():
-                    copy_x(step, base + offset, field, way, source(field, way)).start()
-
-    def pack_rows(step, base, kinds):
-        for offset, (field, way) in enumerate(kinds):
-            row = 0 if way < 0 else cy - 1
-            for x in range(cx):
-                send_y[6 * step + base + offset, pl.ds(x, 1), :] = cur[field, 1 + x, pl.ds(row, 1), :]
-
-    def send_rows(step, base, kinds):
-        pack_rows(step, base, kinds)
-        for offset, (field, way) in enumerate(kinds):
+    def send_x(step, messages, source):
+        for message in messages:
+            @pl.when(edge(message[2], "gx"))
+            def _():
+                copy_x(step, message, source).start()
+
+    def send_rows(step, messages):
+        for message in messages:
+            start, fields, way = message
+
             @pl.when(edge(way, "gy"))
             def _():
-                copy_y(step, base + offset, way).start()
-
-    def finish_sends(step, base, kinds_x, kinds_y):
-        for offset, (field, way) in enumerate(kinds_x):
-            @pl.when(edge(way, "gx"))
-            def _():
-                copy_x(step, base + offset, field, way, layer(field, way)).wait_send()
-        for offset, (field, way) in enumerate(kinds_y):
-            @pl.when(edge(way, "gy"))
-            def _():
-                copy_y(step, base + offset, way).wait_send()
-
-    def receive(step, base, kinds_x, kinds_y):
-        for offset, (field, way) in enumerate(kinds_y):
-            slot = 6 * step + base + offset
+                row = 0 if way < 0 else cy - 1
+                for offset, field in enumerate(fields):
+                    for x in range(cx):
+                        send_y[6 * step + start + offset, pl.ds(x, 1), :] = cur[field, 1 + x, pl.ds(row, 1), :]
+                copy_y(step, message).start()
+
+    def finish_sends(step, messages_x, messages_y):
+        for message in messages_x:
+            @pl.when(edge(message[2], "gx"))
+            def _():
+                copy_x(step, message, layer).wait_send()
+        for message in messages_y:
+            @pl.when(edge(message[2], "gy"))
+            def _():
+                copy_y(step, message).wait_send()
+
+    def receive(step, messages_x, messages_y):
+        for message in messages_y:
+            start, fields, way = message
 
             @pl.when(edge(-way, "gy"))
             def _():
-                copy_y(step, base + offset, way).wait_recv()
+                copy_y(step, message).wait_recv()
 
             @pl.when(jnp.logical_not(edge(-way, "gy")))
             def _():
-                halo_y[slot] = jnp.zeros((cx, cz), jnp.float32)
-        for offset, (field, way) in enumerate(kinds_x):
-            slot = 6 * step + base + offset
+                for offset in range(len(fields)):
+                    halo_y[6 * step + start + offset] = jnp.zeros((cx, cz), jnp.float32)
+        for message in messages_x:
+            start, fields, way = message
             place = cx + 1 if way < 0 else 0
 
             @pl.when(edge(-way, "gx"))
             def _():
-                copy_x(step, base + offset, field, way, layer(field, way)).wait_recv()
-                cur[field, place] = halo_x[slot]
+                copy_x(step, message, layer).wait_recv()
+                for offset, field in enumerate(fields):
+                    cur[field, place] = halo_x[6 * step + start + offset]
 
             @pl.when(jnp.logical_not(edge(-way, "gx")))
             def _():
-                cur[field, place] = jnp.zeros((cy, cz), jnp.float32)
+                for field in fields:
+                    cur[field, place] = jnp.zeros((cy, cz), jnp.float32)
 
     groups = [[], [], [], []]
     half = max(n_x // 2, 1)
@@ -194,12 +202,17 @@
             scaled = COURANT * coef[0, x, rows, :]
             sxy, sxz, syz = tile(SXY, x, t), tile(SXZ, x, t), tile(SYZ, x, t)
             sxx, syy, szz = tile(SXX, x, t), tile(SYY, x, t), tile(SZZ, x, t)
-            cur[VX, x + 1, rows, :] = tile(VX, x, t) - scaled * (
-                (tile(SXX, x + 1, t) - sxx) + (sxy - y_before(sxy, SXY, x, t, slot + 1)) + (sxz - z_before(sxz)))
-            cur[VY, x + 1, rows, :] = tile(VY, x, t) - scaled * (
-                (sxy - tile(SXY, x - 1, t)) + (y_after(syy, SYY, x, t, slot) - syy) + (syz - z_before(syz)))
-            cur[VZ, x + 1, rows, :] = tile(VZ, x, t) - scaled * (
-                (sxz - tile(SXZ, x - 1, t)) + (syz - y_before(syz, SYZ, x, t, slot + 2)) + (z_after(szz) - szz))
+            moved = (
+                tile(VX, x, t) - scaled * (
+                    (tile(SXX, x + 1, t) - sxx) + (sxy - y_before(sxy, SXY, x, t, slot + 1)) + (sxz - z_before(sxz))),
+                tile(VY, x, t) - scaled * (
+                    (sxy - tile(SXY, x - 1, t)) + (y_after(syy, SYY, x, t, slot) - syy) + (syz - z_before(syz))),
+                tile(VZ, x, t) - scaled * (
+                    (sxz - tile(SXZ, x - 1, t)) + (syz - y_before(syz, SYZ, x, t, slot + 2)) + (z_after(szz) - szz)))
+            for field, value in enumerate(moved):
+                cur[field, x + 1, rows, :] = value
+                if step == STEPS - 1:
+                    out[field, x, rows, :] = value
 
     def stress(step, x):
         slot = 6 * step + 3
@@ -217,10 +230,13 @@
                 strain[6 * step + index, x, rows, :] = value
             pull = (COURANT * coef[1, x, rows, :]) * (exx + eyy + ezz)
             mu = COURANT * coef[2, x, rows, :]
-            for index in range(3):
-                cur[SXX + index, x + 1, rows, :] = tile(SXX + index, x, t) - (pull + (2.0 * mu) * both[index])
-            for index in range(3, 6):
-                cur[SXX + index, x + 1, rows, :] = tile(SXX + index, x, t) - mu * both[index]
+            for index, value in enumerate(both):
+                change = pull + (2.0 * mu) * value if index < 3 else mu * value
+                moved = tile(SXX + index, x, t) - change
+                if step == STEPS - 1:
+                    out[SXX + index, x, rows, :] = moved
+                else:
+                    cur[SXX + index, x + 1, rows, :] = moved
 
     def over(first, last, body):
         def run(x, carry):
@@ -236,10 +252,10 @@
 
     for step in range(STEPS):
         if step == 0:
-            send_x(0, 0, STRESS_X, lambda field, way: adj.at[field, 0 if way < 0 else cx - 1], (-1, 1))
+            send_x(0, STRESS_X, first_layer)
             for copy in loads:
                 copy.wait()
-            send_rows(0, 0, STRESS_Y)
+            send_rows(0, STRESS_Y)
             send_group(0)
             def invert(block, carry):
                 total = jnp.int32(0)
@@ -248,32 +264,24 @@
                 inv[block] = total
                 return carry
             lax.fori_loop(0, n_x, invert, 0)
-        receive(step, 0, STRESS_X, STRESS_Y)
+        receive(step, STRESS_X, STRESS_Y)
         if step > 0:
-            finish_sends(step - 1, 3, SPEED_X, SPEED_Y)
+            finish_sends(step - 1, SPEED_X, SPEED_Y)
         ends(functools.partial(velocity, step))
-        send_x(step, 3, SPEED_X, layer, (-1, 1))
+        send_x(step, SPEED_X, layer)
         over(1, cx - 1, functools.partial(velocity, step))
-        send_rows(step, 3, SPEED_Y)
+        send_rows(step, SPEED_Y)
         send_group(1 + 2 * step)
-        if step == STEPS - 1:
-            speed_out = [pltpu.make_async_copy(cur.at[f, pl.ds(1, cx)], out.at[f], out_sem.at[f]) for f in range(3)]
-            for copy in speed_out:
-                copy.start()
-        receive(step, 3, SPEED_X, SPEED_Y)
-        finish_sends(step, 0, STRESS_X, STRESS_Y)
+        receive(step, SPEED_X, SPEED_Y)
+        finish_sends(step, STRESS_X, STRESS_Y)
         ends(functools.partial(stress, step))
         if step < STEPS - 1:
-            send_x(step + 1, 0, STRESS_X, layer, (-1, 1))
+            send_x(step + 1, STRESS_X, layer)
         over(1, cx - 1, functools.partial(stress, step))
         if step < STEPS - 1:
-            send_rows(step + 1, 0, STRESS_Y)
+            send_rows(step + 1, STRESS_Y)
             send_group(2 + 2 * step)
-    finish_sends(STEPS - 1, 3, SPEED_X, SPEED_Y)
-    stress_out = [pltpu.make_async_copy(cur.at[f, pl.ds(1, cx)], out.at[f], out_sem.at[f]) for f in range(3, 9)]
-    for copy in stress_out:
-        copy.start()
-
+    finish_sends(STEPS - 1, SPEED_X, SPEED_Y)
     own_words.wait()
     own_factor.wait()
     for distance in range(1, n_x):
@@ -342,15 +350,10 @@
                     grad_lambda = grad_lambda + (e[0] + e[1] + e[2]) * (f[0] + f[1] + f[2])
                     grad_mu = grad_mu + 2.0 * (e[0] * f[0] + e[1] * f[1] + e[2] * f[2])
                     grad_mu = grad_mu + e[3] * f[3] + e[4] * f[4] + e[5] * f[5]
-                gsum[0, x, rows, columns] = grad_lambda
-                gsum[1, x, rows, columns] = grad_mu
+                grads[0, x, rows, columns] = grad_lambda
+                grads[1, x, rows, columns] = grad_mu
 
     over(0, cx, gradient)
-    grad_out = pltpu.make_async_copy(gsum, grads, loc_sem.at[3])
-    grad_out.start()
-    for copy in speed_out + stress_out:
-        copy.wait()
-    grad_out.wait()
 
 
 def on_device(n_x, n_y, adjoint, buoyancy, lame_lambda, shear_mu, packed, scales, perm):
@@ -360,18 +363,15 @@
     packed = packed.reshape(n_x, comp, segw // lanes, lanes)
     halos = 6 * STEPS
     dma = pltpu.SemaphoreType.DMA
-    any_space = pl.BlockSpec(memory_space=pl.ANY)
     return pl.pallas_call(
         functools.partial(kernel, n_x, n_y),
-        out_shape=(jax.ShapeDtypeStruct(adjoint.shape, jnp.float32),
-                   jax.ShapeDtypeStruct((2, cx, cy, cz), jnp.float32)),
+        out_shape=(pltpu.VMEM(adjoint.shape, jnp.float32), pltpu.VMEM((2, cx, cy, cz), jnp.float32)),
         in_specs=[pl.BlockSpec(memory_space=pltpu.HBM)] * 6 + [pl.BlockSpec(memory_space=pltpu.SMEM)],
-        out_specs=(any_space, any_space),
+        out_specs=(pl.BlockSpec(memory_space=pltpu.VMEM),) * 2,
         scratch_shapes=[
             pltpu.VMEM((fields, cx + 2, cy, cz), jnp.float32),
             pltpu.VMEM((3, cx, cy, cz), jnp.float32),
             pltpu.VMEM((comp, cx, cy, cz), jnp.float32),
-            pltpu.VMEM((2, cx, cy, cz), jnp.float32),
             pltpu.VMEM((halos, cy, cz), jnp.float32),
             pltpu.VMEM((halos, cx, cz), jnp.float32),
             pltpu.VMEM((halos, cx, cz), jnp.float32),
@@ -379,11 +379,11 @@
             pltpu.VMEM((n_x, 1, comp), jnp.float32),
             pltpu.SMEM((n_x, 1, comp), jnp.float32),
             pltpu.SMEM((n_x,), jnp.int32),
-            dma((12,)), dma((9,)), dma((halos,)), dma((halos,)), dma((halos,)), dma((halos,)),
-            dma((n_x,)), dma((n_x,)), dma((n_x,)), dma((n_x,)), dma((4,)),
+            dma((12,)), dma((halos,)), dma((halos,)), dma((halos,)), dma((halos,)),
+            dma((n_x,)), dma((n_x,)), dma((n_x,)), dma((n_x,)), dma((3,)),
         ],
         compiler_params=pltpu.CompilerParams(collective_id=0, has_side_effects=True,
-                                             vmem_limit_bytes=40 * 1024 * 1024),
+                                             vmem_limit_bytes=64000000),
     )(adjoint, buoyancy, lame_lambda, shear_mu, packed, scales, perm)
 
 

time: 36.1 us -> 28.7 us (0.80)
  local copies, waits for them, and re-layouts: 9.18 us -> 2.2 us
    unnamed x16 -> x2, local copies, waits for them, and re-layouts: 9.18 us -> 2.2 us
where the time goes in v2:
time: 28.7 us; the launch traced here: 28.6 us
  Pallas kernels  25.7 us (90%)
  local copies, waits for them, and re-layouts  2.2 us (8%)
  between operations  0.64 us (2%)
    pallas_call x1, Pallas kernels, on_device(): pl.pallas_call(functools.partial(kernel, n_x, n_y), out_shape=(pltpu.VMEM...  25.7 us
    unnamed x2, local copies, waits for them, and re-layouts  2.2 us

profile of v2, /device:TPU:1, one launch (start us, length us, event | category | flops | bytes accessed | tf_op | source)
XLA Modules:
  0.0 28.6 jit_solution(12395375729810057555)
XLA Ops:
  0.6 25.7 %shard_map.86 = (f32[9,4,32,512]{3,2,1,0:T(8,128)S(1)}, f32[2,4,32,512]{3,2,1,0:T(8,128)S(1)}) custom-call(f32[9,4,32,512]{3,2,1,0:T(8,128)} %adj.1, f32[4,32,512]{2,1,0:T(8,128)} %buoy.1, f32[4,32,512]{2,1,0:T(8,128)} %lam.1, f32[4,32,512]{2,1,0:T(8,128)} %shear.1, s32[8,12,16,128]{3,2,1,0:T(8,128)} %bitcast.1, f32[1,8,1,12]{3,2,1,0:T(1,128)} %scales.1, ...), custom_call_target="tpu_custom_call" | custom-call | tf_op jit(solution)/shard_map/pallas_call | solution.py:366
  26.4 1.4 %copy.11 = f32[9,4,32,512]{3,2,1,0:T(8,128)} copy(f32[9,4,32,512]{3,2,1,0:T(8,128)S(1)} %get-tuple-element.2) | data formatting | bytes 4718592
  27.8 0.8 %copy.12 = f32[2,4,32,512]{3,2,1,0:T(8,128)} copy(f32[2,4,32,512]{3,2,1,0:T(8,128)S(1)} %get-tuple-element.3) | data formatting | bytes 1048576

commit v3 on v2

--- a/solution.py
+++ b/solution.py
@@ -11,6 +11,7 @@
 STEPS = 2
 COURANT = 0.15
 ROWS = 8
+PIECES = 2
 
 VX, VY, VZ, SXX, SYY, SZZ, SXY, SXZ, SYZ = range(9)
 
@@ -32,13 +33,16 @@
 
 
 def kernel(n_x, n_y, adj, buoy, lam, shear, packed, scales, perm, out, grads,
-           cur, coef, strain, halo_x, halo_y, send_y, words, factors, factor_s, inv,
-           in_sem, xs_sem, xr_sem, ys_sem, yr_sem, ws_sem, wr_sem, fs_sem, fr_sem, loc_sem):
+           cur, coef, strain, halo_x, halo_y, send_y, factors, factor_s, inv,
+           in_sem, xs_sem, xr_sem, ys_sem, yr_sem, ws_sem, wr_sem, fs_sem, fr_sem, loc_sem, *words):
     cx, cy, cz = buoy.shape
     comp = packed.shape[1]
+    per_step = comp // STEPS
     lanes = packed.shape[3]
     segw = packed.shape[2] * lanes
     tiles = cy // ROWS
+    pieces = xs_sem.shape[1]
+    part = cy // pieces
     me_x, me_y = lax.axis_index("gx"), lax.axis_index("gy")
 
     loads = []
@@ -46,11 +50,13 @@
         loads.append(pltpu.make_async_copy(adj.at[index], cur.at[index, pl.ds(1, cx)], in_sem.at[index]))
     for index, ref in enumerate((buoy, lam, shear)):
         loads.append(pltpu.make_async_copy(ref, coef.at[index], in_sem.at[9 + index]))
-    own_words = pltpu.make_async_copy(packed.at[me_x], words.at[me_x], loc_sem.at[0])
+    own_words = [pltpu.make_async_copy(packed.at[me_x, pl.ds(step * per_step, per_step)], words[step].at[me_x],
+                                       loc_sem.at[2 + step]) for step in range(STEPS)]
     own_factor = pltpu.make_async_copy(scales.at[0, me_x], factors.at[me_x], loc_sem.at[1])
     for copy in loads:
         copy.start()
-    own_words.start()
+    for copy in own_words:
+        copy.start()
     own_factor.start()
 
     barrier = pltpu.get_barrier_semaphore()
@@ -68,12 +74,13 @@
 
     pl.semaphore_wait(barrier, n_x - 1 + jnp.minimum(me_y, 1) + jnp.minimum(n_y - 1 - me_y, 1))
 
-    def copy_x(step, message, source):
+    def copy_x(step, message, source, piece):
         start, fields, way = message
         slot = 6 * step + start
         return pltpu.make_async_remote_copy(
-            src_ref=source(fields, way), dst_ref=halo_x.at[pl.ds(slot, len(fields))],
-            send_sem=xs_sem.at[slot], recv_sem=xr_sem.at[slot],
+            src_ref=source(fields, way, piece),
+            dst_ref=halo_x.at[pl.ds(slot, len(fields)), pl.ds(piece * part, part)],
+            send_sem=xs_sem.at[slot, piece], recv_sem=xr_sem.at[slot, piece],
             device_id={"gx": me_x + way}, device_id_type=MESH)
 
     def copy_y(step, message):
@@ -84,17 +91,18 @@
             send_sem=ys_sem.at[slot], recv_sem=yr_sem.at[slot],
             device_id={"gy": me_y + way}, device_id_type=MESH)
 
-    def layer(fields, way):
-        return cur.at[pl.ds(fields[0], len(fields)), 1 if way < 0 else cx]
-
-    def first_layer(fields, way):
-        return adj.at[pl.ds(fields[0], len(fields)), 0 if way < 0 else cx - 1]
-
-    def word_copy(distance):
+    def layer(fields, way, piece):
+        return cur.at[pl.ds(fields[0], len(fields)), 1 if way < 0 else cx, pl.ds(piece * part, part)]
+
+    def first_layer(fields, way, piece):
+        return adj.at[pl.ds(fields[0], len(fields)), 0 if way < 0 else cx - 1, pl.ds(piece * part, part)]
+
+    def word_copy(distance, step):
         to = partner(me_x, distance, n_x)
+        stored = pl.ds(step * per_step, per_step)
         return pltpu.make_async_remote_copy(
-            src_ref=packed.at[to], dst_ref=words.at[me_x], send_sem=ws_sem.at[distance],
-            recv_sem=wr_sem.at[distance], device_id={"gx": to}, device_id_type=MESH)
+            src_ref=packed.at[to, stored], dst_ref=words[step].at[me_x], send_sem=ws_sem.at[distance, step],
+            recv_sem=wr_sem.at[distance, step], device_id={"gx": to}, device_id_type=MESH)
 
     def factor_copy(distance):
         to = partner(me_x, distance, n_x)
@@ -102,11 +110,11 @@
             src_ref=scales.at[0, to], dst_ref=factors.at[me_x], send_sem=fs_sem.at[distance],
             recv_sem=fr_sem.at[distance], device_id={"gx": to}, device_id_type=MESH)
 
-    def send_x(step, messages, source):
+    def send_x(step, messages, source, piece):
         for message in messages:
             @pl.when(edge(message[2], "gx"))
             def _():
-                copy_x(step, message, source).start()
+                copy_x(step, message, source, piece).start()
 
     def send_rows(step, messages):
         for message in messages:
@@ -124,14 +132,15 @@
         for message in messages_x:
             @pl.when(edge(message[2], "gx"))
             def _():
-                copy_x(step, message, layer).wait_send()
+                for piece in range(pieces):
+                    copy_x(step, message, layer, piece).wait_send()
         for message in messages_y:
             @pl.when(edge(message[2], "gy"))
             def _():
                 copy_y(step, message).wait_send()
 
-    def receive(step, messages_x, messages_y):
-        for message in messages_y:
+    def receive_y(step, messages):
+        for message in messages:
             start, fields, way = message
 
             @pl.when(edge(-way, "gy"))
@@ -142,36 +151,48 @@
             def _():
                 for offset in range(len(fields)):
                     halo_y[6 * step + start + offset] = jnp.zeros((cx, cz), jnp.float32)
-        for message in messages_x:
+
+    def receive_x(step, messages, piece):
+        rows = pl.ds(piece * part, part)
+        for message in messages:
             start, fields, way = message
             place = cx + 1 if way < 0 else 0
 
             @pl.when(edge(-way, "gx"))
             def _():
-                copy_x(step, message, layer).wait_recv()
+                copy_x(step, message, layer, piece).wait_recv()
                 for offset, field in enumerate(fields):
-                    cur[field, place] = halo_x[6 * step + start + offset]
+                    cur[field, place, rows, :] = halo_x[6 * step + start + offset, rows, :]
 
             @pl.when(jnp.logical_not(edge(-way, "gx")))
             def _():
                 for field in fields:
-                    cur[field, place] = jnp.zeros((cy, cz), jnp.float32)
-
-    groups = [[], [], [], []]
-    half = max(n_x // 2, 1)
-    for distance in range(1, n_x):
-        if distance >= half:
-            where = 0 if n_x < 8 else (1 if distance == half else 2 + (distance % 2))
-        else:
-            where = distance % 2
-        if n_x == 8:
-            where = {1: 0, 2: 0, 4: 0, 3: 1, 5: 1, 6: 2, 7: 3}[distance]
-        groups[where].append(distance)
+                    cur[field, place, rows, :] = jnp.zeros((part, cz), jnp.float32)
+
+    far = max(3 * n_x // 4, 1)
 
     def send_group(which):
-        for distance in groups[which]:
-            factor_copy(distance).start()
-            word_copy(distance).start()
+        step, late = which // 2, which % 2
+        for distance in range(2, n_x) if n_x > 2 else ():
+            if (distance >= far) == (late == 1):
+                word_copy(distance, step).start()
+        if late == 1:
+            word_copy(1, step).start()
+        if which == 0:
+            for distance in range(1, n_x):
+                factor_copy(distance).start()
+
+    def receive_words(step):
+        if step == 0:
+            own_factor.wait()
+            for distance in range(1, n_x):
+                factor_copy(distance).wait()
+            to_scalar = pltpu.make_async_copy(factors, factor_s, loc_sem.at[0])
+            to_scalar.start()
+            to_scalar.wait()
+        own_words[step].wait()
+        for distance in range(1, n_x):
+            word_copy(distance, step).wait()
 
     sub = lax.broadcasted_iota(jnp.int32, (ROWS, cz), 0)
     lane = lax.broadcasted_iota(jnp.int32, (ROWS, cz), 1)
@@ -195,9 +216,9 @@
         row = halo_y[slot, pl.ds(x, 1), :] if t == tiles - 1 else cur[field, x + 1, pl.ds(t * ROWS + ROWS, 1), :]
         return jnp.where(last_row, jnp.broadcast_to(row, value.shape), pltpu.roll(value, ROWS - 1, 0))
 
-    def velocity(step, x):
+    def velocity(step, which, x):
         slot = 6 * step
-        for t in range(tiles):
+        for t in which:
             rows = pl.ds(t * ROWS, ROWS)
             scaled = COURANT * coef[0, x, rows, :]
             sxy, sxz, syz = tile(SXY, x, t), tile(SXZ, x, t), tile(SYZ, x, t)
@@ -214,9 +235,9 @@
                 if step == STEPS - 1:
                     out[field, x, rows, :] = value
 
-    def stress(step, x):
+    def stress(step, which, x):
         slot = 6 * step + 3
-        for t in range(tiles):
+        for t in which:
             rows = pl.ds(t * ROWS, ROWS)
             vx, vy, vz = tile(VX, x, t), tile(VY, x, t), tile(VZ, x, t)
             exx = vx - tile(VX, x - 1, t)
@@ -250,48 +271,6 @@
             return carry
         lax.fori_loop(0, 2, run, 0)
 
-    for step in range(STEPS):
-        if step == 0:
-            send_x(0, STRESS_X, first_layer)
-            for copy in loads:
-                copy.wait()
-            send_rows(0, STRESS_Y)
-            send_group(0)
-            def invert(block, carry):
-                total = jnp.int32(0)
-                for holder in range(n_x):
-                    total = jnp.where(perm[0, holder] == block, holder, total)
-                inv[block] = total
-                return carry
-            lax.fori_loop(0, n_x, invert, 0)
-        receive(step, STRESS_X, STRESS_Y)
-        if step > 0:
-            finish_sends(step - 1, SPEED_X, SPEED_Y)
-        ends(functools.partial(velocity, step))
-        send_x(step, SPEED_X, layer)
-        over(1, cx - 1, functools.partial(velocity, step))
-        send_rows(step, SPEED_Y)
-        send_group(1 + 2 * step)
-        receive(step, SPEED_X, SPEED_Y)
-        finish_sends(step, STRESS_X, STRESS_Y)
-        ends(functools.partial(stress, step))
-        if step < STEPS - 1:
-            send_x(step + 1, STRESS_X, layer)
-        over(1, cx - 1, functools.partial(stress, step))
-        if step < STEPS - 1:
-            send_rows(step + 1, STRESS_Y)
-            send_group(2 + 2 * step)
-    finish_sends(STEPS - 1, SPEED_X, SPEED_Y)
-    own_words.wait()
-    own_factor.wait()
-    for distance in range(1, n_x):
-        factor_copy(distance).wait()
-    to_scalar = pltpu.make_async_copy(factors, factor_s, loc_sem.at[2])
-    to_scalar.start()
-    for distance in range(1, n_x):
-        word_copy(distance).wait()
-    to_scalar.wait()
-
     width = lanes
     per_x = cy * cz // (4 * segw)
 
@@ -302,7 +281,7 @@
 
     sub_w = lax.broadcasted_iota(jnp.int32, (ROWS, width), 0)
 
-    def gradient(x):
+    def gradient(step, x):
         made = {}
         for t in range(tiles):
             for chunk in range(cz // width):
@@ -330,7 +309,7 @@
                         word = None
                         for position, (block, start) in enumerate(distinct):
                             piece = jnp.broadcast_to(
-                                words[holders[block], c, pl.ds(start // lanes, 1), :], (ROWS, width))
+                                words[step][holders[block], c - per_step * step, pl.ds(start // lanes, 1), :], (ROWS, width))
                             word = piece if word is None else jnp.where(masks[position - 1], piece, word)
                         made[key, c] = word ^ jnp.int32(-2147483648)
                     byte = (lax.shift_right_logical(made[key, c], shift) & 255) - 128
@@ -342,18 +321,68 @@
                             factor = jnp.where(sub_w >= r, factor_s[holders[blocks[r]], 0, c], factor)
                     return byte.astype(jnp.float32) * factor
 
-                grad_lambda = jnp.zeros((ROWS, width), jnp.float32)
-                grad_mu = jnp.zeros((ROWS, width), jnp.float32)
-                for step in range(comp // 6):
-                    e = [strain[6 * step + index, x, rows, columns] for index in range(6)]
-                    f = [stored(6 * step + index) for index in range(6)]
-                    grad_lambda = grad_lambda + (e[0] + e[1] + e[2]) * (f[0] + f[1] + f[2])
-                    grad_mu = grad_mu + 2.0 * (e[0] * f[0] + e[1] * f[1] + e[2] * f[2])
-                    grad_mu = grad_mu + e[3] * f[3] + e[4] * f[4] + e[5] * f[5]
+                e = [strain[6 * step + index, x, rows, columns] for index in range(6)]
+                f = [stored(6 * step + index) for index in range(6)]
+                grad_lambda = (e[0] + e[1] + e[2]) * (f[0] + f[1] + f[2])
+                grad_mu = 2.0 * (e[0] * f[0] + e[1] * f[1] + e[2] * f[2])
+                grad_mu = grad_mu + e[3] * f[3] + e[4] * f[4] + e[5] * f[5]
+                if step > 0:
+                    grad_lambda = grads[0, x, rows, columns] + grad_lambda
+                    grad_mu = grads[1, x, rows, columns] + grad_mu
                 grads[0, x, rows, columns] = grad_lambda
                 grads[1, x, rows, columns] = grad_mu
 
-    over(0, cx, gradient)
+    def inside(piece):
+        return range(piece * part // ROWS, (piece + 1) * part // ROWS)
+
+    outer = (0, tiles - 1) if tiles > 1 else (0,)
+    inner = range(1, tiles - 1)
+
+    for step in range(STEPS):
+        if step == 0:
+            for piece in range(pieces):
+                send_x(0, STRESS_X, first_layer, piece)
+            for copy in loads:
+                copy.wait()
+            send_rows(0, STRESS_Y)
+            send_group(0)
+            def invert(block, carry):
+                total = jnp.int32(0)
+                for holder in range(n_x):
+                    total = jnp.where(perm[0, holder] == block, holder, total)
+                inv[block] = total
+                return carry
+            lax.fori_loop(0, n_x, invert, 0)
+        if step > 0:
+            finish_sends(step - 1, SPEED_X, SPEED_Y)
+        receive_y(step, STRESS_Y)
+        for piece in range(pieces):
+            receive_x(step, STRESS_X, piece)
+            ends(functools.partial(velocity, step, inside(piece)))
+            send_x(step, SPEED_X, layer, piece)
+        over(1, cx - 1, functools.partial(velocity, step, outer))
+        send_rows(step, SPEED_Y)
+        over(1, cx - 1, functools.partial(velocity, step, inner))
+        send_group(1 + 2 * step)
+        if step > 0:
+            receive_words(step - 1)
+            over(0, cx, functools.partial(gradient, step - 1))
+        finish_sends(step, STRESS_X, STRESS_Y)
+        receive_y(step, SPEED_Y)
+        for piece in range(pieces):
+            receive_x(step, SPEED_X, piece)
+            ends(functools.partial(stress, step, inside(piece)))
+            if step < STEPS - 1:
+                send_x(step + 1, STRESS_X, layer, piece)
+        over(1, cx - 1, functools.partial(stress, step, outer))
+        if step < STEPS - 1:
+            send_rows(step + 1, STRESS_Y)
+        over(1, cx - 1, functools.partial(stress, step, inner))
+        if step < STEPS - 1:
+            send_group(2 + 2 * step)
+    finish_sends(STEPS - 1, SPEED_X, SPEED_Y)
+    receive_words(STEPS - 1)
+    over(0, cx, functools.partial(gradient, STEPS - 1))
 
 
 def on_device(n_x, n_y, adjoint, buoyancy, lame_lambda, shear_mu, packed, scales, perm):
@@ -362,6 +391,7 @@
     lanes = min(128, segw)
     packed = packed.reshape(n_x, comp, segw // lanes, lanes)
     halos = 6 * STEPS
+    pieces = PIECES if cy % (PIECES * ROWS) == 0 else 1
     dma = pltpu.SemaphoreType.DMA
     return pl.pallas_call(
         functools.partial(kernel, n_x, n_y),
@@ -375,13 +405,12 @@
             pltpu.VMEM((halos, cy, cz), jnp.float32),
             pltpu.VMEM((halos, cx, cz), jnp.float32),
             pltpu.VMEM((halos, cx, cz), jnp.float32),
-            pltpu.VMEM((n_x, comp, segw // lanes, lanes), jnp.int32),
             pltpu.VMEM((n_x, 1, comp), jnp.float32),
             pltpu.SMEM((n_x, 1, comp), jnp.float32),
             pltpu.SMEM((n_x,), jnp.int32),
-            dma((12,)), dma((halos,)), dma((halos,)), dma((halos,)), dma((halos,)),
-            dma((n_x,)), dma((n_x,)), dma((n_x,)), dma((n_x,)), dma((3,)),
-        ],
+            dma((12,)), dma((halos, pieces)), dma((halos, pieces)), dma((halos,)), dma((halos,)),
+            dma((n_x, STEPS)), dma((n_x, STEPS)), dma((n_x,)), dma((n_x,)), dma((2 + STEPS,)),
+        ] + [pltpu.VMEM((n_x, comp // STEPS, segw // lanes, lanes), jnp.int32)] * STEPS,
         compiler_params=pltpu.CompilerParams(collective_id=0, has_side_effects=True,
                                              vmem_limit_bytes=64000000),
     )(adjoint, buoyancy, lame_lambda, shear_mu, packed, scales, perm)

time: 28.7 us -> 27.1 us (0.944)
  Pallas kernels: 25.7 us -> 24.1 us
    pallas_call x1, Pallas kernels: 25.7 us -> 24.1 us  [on_device(): pl.pallas_call(functools.partial(kernel, n_x, n_y), out_shape=(pltpu.VMEM...]
where the time goes in v3:
time: 27.1 us; the launch traced here: 26.9 us
  Pallas kernels  24.1 us (89%)
  local copies, waits for them, and re-layouts  2.2 us (8%)
  between operations  0.64 us (2%)
    pallas_call x1, Pallas kernels, on_device(): pl.pallas_call(functools.partial(kernel, n_x, n_y), out_shape=(pltpu.VMEM...  24.1 us
    unnamed x2, local copies, waits for them, and re-layouts  2.2 us

profile of v3, /device:TPU:1, one launch (start us, length us, event | category | flops | bytes accessed | tf_op | source)
XLA Modules:
  0.0 26.9 jit_solution(5183668970919429755)
XLA Ops:
  0.6 24.1 %shard_map.86 = (f32[9,4,32,512]{3,2,1,0:T(8,128)S(1)}, f32[2,4,32,512]{3,2,1,0:T(8,128)S(1)}) custom-call(f32[9,4,32,512]{3,2,1,0:T(8,128)} %adj.1, f32[4,32,512]{2,1,0:T(8,128)} %buoy.1, f32[4,32,512]{2,1,0:T(8,128)} %lam.1, f32[4,32,512]{2,1,0:T(8,128)} %shear.1, s32[8,12,16,128]{3,2,1,0:T(8,128)} %bitcast.1, f32[1,8,1,12]{3,2,1,0:T(1,128)} %scales.1, ...), custom_call_target="tpu_custom_call" | custom-call | tf_op jit(solution)/shard_map/pallas_call | solution.py:396
  24.7 1.4 %copy.11 = f32[9,4,32,512]{3,2,1,0:T(8,128)} copy(f32[9,4,32,512]{3,2,1,0:T(8,128)S(1)} %get-tuple-element.2) | data formatting | bytes 4718592
  26.1 0.8 %copy.12 = f32[2,4,32,512]{3,2,1,0:T(8,128)} copy(f32[2,4,32,512]{3,2,1,0:T(8,128)S(1)} %get-tuple-element.3) | data formatting | bytes 1048576
